TPU v7x, 32 devices: a 4x4x1 block of a 4x4x8 slice. The times are simulated.
32 devices in a mesh: pair: 1 (over z), tp: 4 (over y), side: 8 (over x, core).
Axes of the slice: x: 4, y: 4, z: 1, core: 2. Of those that a mesh axis runs over, the one named last changes fastest.
The devices are a block of a 4x4x8 slice.
Arguments:
- x: bfloat16 [2048, 2048], P(('pair', 'side'))
- req_len: int32 [8], P('pair')
- dest: int32 [8], P('pair')
- w_qkv: bfloat16 [2, 2048, 3072], replicated
- w_out: bfloat16 [2, 2048, 2048], replicated
- w_gate: bfloat16 [2, 2048, 8192], replicated
- w_up: bfloat16 [2, 2048, 8192], replicated
- w_down: bfloat16 [2, 8192, 2048], replicated
- y_tok: bfloat16 [8, 64, 2048], P(('pair', 'side'))
- k_cache: bfloat16 [8, 2, 64, 128, 8, 64], P(('pair', 'side'), None, None, None, 'tp')
- v_cache: bfloat16 [8, 2, 64, 128, 8, 64], P(('pair', 'side'), None, None, None, 'tp')
- c_len: int32 [8, 64], P(('pair', 'side'))
Outputs:
- output 1: bfloat16 [2048, 2048], P(('pair', 'side'))
- output 2: bfloat16 [8, 64, 2048], P(('pair', 'side'))
- output 3: bfloat16 [8, 2, 448, 8, 64], P(('pair', 'side'), None, None, 'tp')
- output 4: bfloat16 [8, 2, 448, 8, 64], P(('pair', 'side'), None, None, 'tp')
- output 5: bfloat16 [8, 2, 64, 128, 8, 64], P(('pair', 'side'), None, None, None, 'tp')
- output 6: bfloat16 [8, 2, 64, 128, 8, 64], P(('pair', 'side'), None, None, None, 'tp')
All inputs are finite; a program needn't handle non-finite values.
Results may differ from a plain program's by a relative error of at most 0.0173637.
Values are sent between devices in bfloat16 or wider.
A program may use at most 768 MiB of HBM per device.

v0:
```python
import jax
import jax.numpy as jnp
from jax import lax
from jax.sharding import PartitionSpec as P

ROPE_BASE = 10000.0
NORM_EPS = 1e-5


def rms_norm(hidden):
    wide_vals = hidden.astype(jnp.float32)
    norm_scale = lax.rsqrt(jnp.mean(wide_vals * wide_vals, axis=-1, keepdims=True) + NORM_EPS)
    return (wide_vals * norm_scale).astype(jnp.bfloat16)


def rotary(vectors, positions):
    half_dim = vectors.shape[-1] // 2
    inv_freq = ROPE_BASE ** (-jnp.arange(half_dim, dtype=jnp.float32) / half_dim)
    angles = positions.astype(jnp.float32)[:, None, None] * inv_freq
    cos_val = jnp.cos(angles)
    sin_val = jnp.sin(angles)
    wide_vals = vectors.astype(jnp.float32)
    lead_half = wide_vals[..., :half_dim]
    tail_half = wide_vals[..., half_dim:]
    return jnp.concatenate([lead_half * cos_val - tail_half * sin_val, tail_half * cos_val + lead_half * sin_val], axis=-1).astype(jnp.bfloat16)


def head_columns(block, groups, tp_size, tp_idx, interleaved):
    row_count, col_count = block.shape
    group_width = col_count // groups
    local_groups = groups // tp_size
    if interleaved:
        head_view = block.reshape(row_count, local_groups, tp_size, group_width)
        return lax.dynamic_index_in_dim(head_view, tp_idx, axis=2, keepdims=False).reshape(row_count, local_groups * group_width)
    return lax.dynamic_slice_in_dim(block, tp_idx * local_groups * group_width, local_groups * group_width, axis=1)


def head_rows(block, groups, tp_size, tp_idx, interleaved):
    row_count, col_count = block.shape
    group_height = row_count // groups
    local_groups = groups // tp_size
    if interleaved:
        head_view = block.reshape(local_groups, tp_size, group_height, col_count)
        return lax.dynamic_index_in_dim(head_view, tp_idx, axis=1, keepdims=False).reshape(local_groups * group_height, col_count)
    return lax.dynamic_slice_in_dim(block, tp_idx * local_groups * group_height, local_groups * group_height, axis=0)


def layer_weights(w_qkv, w_out, w_gate, w_up, w_down, layer, kv_heads, tp_size, tp_idx, interleaved):
    q_cols = w_out.shape[1]
    kv_cols = (w_qkv.shape[2] - q_cols) // 2
    qkv_l = w_qkv[layer]
    wq_l = head_columns(qkv_l[:, :q_cols], kv_heads, tp_size, tp_idx, interleaved)
    wk_l = head_columns(qkv_l[:, q_cols:q_cols + kv_cols], kv_heads, tp_size, tp_idx, interleaved)
    wv_l = head_columns(qkv_l[:, q_cols + kv_cols:], kv_heads, tp_size, tp_idx, interleaved)
    wo_l = head_rows(w_out[layer], kv_heads, tp_size, tp_idx, interleaved)
    ff_local = w_gate.shape[2] // tp_size
    wg_l = lax.dynamic_slice_in_dim(w_gate[layer], tp_idx * ff_local, ff_local, axis=1)
    wu_l = lax.dynamic_slice_in_dim(w_up[layer], tp_idx * ff_local, ff_local, axis=1)
    wd_l = lax.dynamic_slice_in_dim(w_down[layer], tp_idx * ff_local, ff_local, axis=0)
    return wq_l, wk_l, wv_l, wo_l, wg_l, wu_l, wd_l


def project(hidden, wq_l, wk_l, wv_l, positions, kv_local, group_rep):
    row_count = hidden.shape[0]
    head_dim = wk_l.shape[1] // kv_local
    normed = rms_norm(hidden)
    query = jnp.dot(normed, wq_l, preferred_element_type=jnp.float32).astype(jnp.bfloat16)
    key_new = jnp.dot(normed, wk_l, preferred_element_type=jnp.float32).astype(jnp.bfloat16)
    value_new = jnp.dot(normed, wv_l, preferred_element_type=jnp.float32).astype(jnp.bfloat16)
    query = rotary(query.reshape(row_count, kv_local * group_rep, head_dim), positions)
    key_new = rotary(key_new.reshape(row_count, kv_local, head_dim), positions)
    return query.reshape(row_count, kv_local, group_rep, head_dim), key_new, value_new.reshape(row_count, kv_local, head_dim)


def finish_layer(hidden, context, wo_l, wg_l, wu_l, wd_l):
    attn_out = lax.psum(jnp.dot(context, wo_l, preferred_element_type=jnp.float32), 'tp').astype(jnp.bfloat16)
    hidden = (hidden.astype(jnp.float32) + attn_out.astype(jnp.float32)).astype(jnp.bfloat16)
    normed = rms_norm(hidden)
    gate = jnp.dot(normed, wg_l, preferred_element_type=jnp.float32).astype(jnp.bfloat16)
    upper = jnp.dot(normed, wu_l, preferred_element_type=jnp.float32).astype(jnp.bfloat16)
    activated = (jax.nn.silu(gate.astype(jnp.float32)) * upper.astype(jnp.float32)).astype(jnp.bfloat16)
    down = lax.psum(jnp.dot(activated, wd_l, preferred_element_type=jnp.float32), 'tp').astype(jnp.bfloat16)
    return (hidden.astype(jnp.float32) + down.astype(jnp.float32)).astype(jnp.bfloat16)


def prompt_attention(query, key_new, value_new, allowed):
    score_scale = query.shape[-1] ** -0.5
    scores = jnp.einsum('sjrd,tjd->jrst', query, key_new, preferred_element_type=jnp.float32) * score_scale
    scores = jnp.where(allowed, scores, -1e30)
    attn_prob = jax.nn.softmax(scores, axis=-1).astype(jnp.bfloat16)
    context = jnp.einsum('jrst,tjd->sjrd', attn_prob, value_new, preferred_element_type=jnp.float32).astype(jnp.bfloat16)
    return context.reshape(query.shape[0], -1)


def decode_attention(query, k_layer, v_layer, lengths):
    score_scale = query.shape[-1] ** -0.5
    cache_pos = jnp.arange(k_layer.shape[1])
    visible = cache_pos[None, :] <= lengths[:, None]
    scores = jnp.einsum('bjrd,btjd->bjrt', query, k_layer, preferred_element_type=jnp.float32) * score_scale
    scores = jnp.where(visible[:, None, None, :], scores, -1e30)
    attn_prob = jax.nn.softmax(scores, axis=-1).astype(jnp.bfloat16)
    context = jnp.einsum('bjrt,btjd->bjrd', attn_prob, v_layer, preferred_element_type=jnp.float32).astype(jnp.bfloat16)
    return context.reshape(query.shape[0], -1)


def write_slot(cache, row_new, lengths):
    return jax.vmap(lambda one_cache, one_row, one_len: lax.dynamic_update_slice_in_dim(one_cache, one_row[None], one_len, axis=0))(cache, row_new, lengths)


def segments(req_len, seq_len):
    row_ids = jnp.arange(seq_len)
    past_end = row_ids[:, None] >= jnp.cumsum(req_len)[None, :]
    seg_id = jnp.sum(past_end.astype(jnp.int32), axis=1)
    positions = row_ids - jnp.sum(jnp.where(past_end, req_len[None, :], 0), axis=1)
    allowed = (seg_id[:, None] == seg_id[None, :]) & (row_ids[None, :] <= row_ids[:, None])
    return positions, allowed


def pick_interleaved(full, tp_size, tp_idx):
    shape_in = full.shape
    head_view = full.reshape(shape_in[:2] + (shape_in[2] // tp_size, tp_size) + shape_in[3:])
    return lax.dynamic_index_in_dim(head_view, tp_idx, axis=3, keepdims=False)


def request_pieces(full, req_len, dest, max_req):
    side_size = req_len.shape[0]
    starts = jnp.cumsum(req_len) - req_len
    match = dest[None, :] == jnp.arange(side_size)[:, None]
    start_of = jnp.sum(jnp.where(match, starts[None, :], 0), axis=1)
    length_of = jnp.sum(jnp.where(match, req_len[None, :], 0), axis=1)
    padded = jnp.concatenate([full, jnp.zeros((full.shape[0], max_req) + full.shape[2:], full.dtype)], axis=1)

    def one_group(start_row, length):
        piece = lax.dynamic_slice_in_dim(padded, start_row, max_req, axis=1)
        keep = (jnp.arange(max_req) < length)[None, :, None, None]
        return jnp.where(keep, piece, jnp.zeros_like(piece))

    return jax.vmap(one_group)(start_of, length_of)


def solution(mesh):
    tp_size = mesh.shape['tp']
    side_size = mesh.shape['side']
    rows_spec = P(('pair', 'side'), None)
    batch_spec = P(('pair', 'side'), None, None)
    cache_spec = P(('pair', 'side'), None, None, None, 'tp', None)
    prompt_spec = P(('pair', 'side'), None, None, 'tp', None)

    def local_step(x_loc, req_len, dest, w_qkv, w_out, w_gate, w_up, w_down, y_loc, kc_loc, vc_loc, clen_loc):
        side_idx = lax.axis_index('side')
        tp_idx = lax.axis_index('tp')
        layers = w_qkv.shape[0]
        head_dim = kc_loc.shape[-1]
        kv_local = kc_loc.shape[-2]
        kv_heads = kv_local * tp_size
        group_rep = w_out.shape[1] // head_dim // kv_heads
        prompt_rows, model_dim = x_loc.shape
        seq_len = prompt_rows * side_size
        max_req = 2 * prompt_rows - prompt_rows // 4

        x_full = lax.all_gather(x_loc, 'side', axis=0, tiled=True)
        positions, allowed = segments(req_len, seq_len)

        def run_prefill(x_rows):
            hidden = x_rows
            keys_all = []
            values_all = []
            for layer in range(layers):
                wq_l, wk_l, wv_l, wo_l, wg_l, wu_l, wd_l = layer_weights(w_qkv, w_out, w_gate, w_up, w_down, layer, kv_heads, tp_size, tp_idx, False)
                query, key_new, value_new = project(hidden, wq_l, wk_l, wv_l, positions, kv_local, group_rep)
                keys_all.append(key_new)
                values_all.append(value_new)
                context = prompt_attention(query, key_new, value_new, allowed)
                hidden = finish_layer(hidden, context, wo_l, wg_l, wu_l, wd_l)
            return hidden, jnp.stack(keys_all), jnp.stack(values_all)

        def skip_prefill(x_rows):
            kv_shape = (layers, seq_len, kv_local, head_dim)
            return jnp.zeros_like(x_rows), jnp.zeros(kv_shape, jnp.bfloat16), jnp.zeros(kv_shape, jnp.bfloat16)

        hidden, keys_loc, values_loc = lax.cond(side_idx == 0, run_prefill, skip_prefill, x_full)
        keys_full = lax.all_gather(keys_loc, 'tp', axis=2, tiled=True)
        values_full = lax.all_gather(values_loc, 'tp', axis=2, tiled=True)
        k_send = request_pieces(pick_interleaved(keys_full, tp_size, tp_idx), req_len, dest, max_req)
        v_send = request_pieces(pick_interleaved(values_full, tp_size, tp_idx), req_len, dest, max_req)
        k_recv = lax.all_to_all(k_send, 'side', 0, 0, tiled=True)[0]
        v_recv = lax.all_to_all(v_send, 'side', 0, 0, tiled=True)[0]
        hidden_rows = lax.all_to_all(hidden.reshape(side_size, prompt_rows, model_dim), 'side', 0, 0, tiled=True)[0]

        lengths = clen_loc[0]
        hidden_dec = y_loc[0]
        k_out = []
        v_out = []
        for layer in range(layers):
            wq_l, wk_l, wv_l, wo_l, wg_l, wu_l, wd_l = layer_weights(w_qkv, w_out, w_gate, w_up, w_down, layer, kv_heads, tp_size, tp_idx, True)
            query, key_new, value_new = project(hidden_dec, wq_l, wk_l, wv_l, lengths, kv_local, group_rep)
            k_layer = write_slot(kc_loc[0, layer], key_new, lengths)
            v_layer = write_slot(vc_loc[0, layer], value_new, lengths)
            context = decode_attention(query, k_layer, v_layer, lengths)
            hidden_dec = finish_layer(hidden_dec, context, wo_l, wg_l, wu_l, wd_l)
            k_out.append(k_layer)
            v_out.append(v_layer)
        return hidden_rows, hidden_dec[None], k_recv[None], v_recv[None], jnp.stack(k_out)[None], jnp.stack(v_out)[None]

    return jax.shard_map(local_step, mesh=mesh,
                         in_specs=(rows_spec, P('pair'), P('pair'), P(), P(), P(), P(), P(), batch_spec, cache_spec, cache_spec, rows_spec),
                         out_specs=(rows_spec, batch_spec, prompt_spec, prompt_spec, cache_spec, cache_spec),
                         check_vma=False)
```

profile of v0, /device:TPU:98, one launch (start us, length us, event | category | flops | bytes accessed | tf_op | source)
XLA Modules:
  0.0 3640.7 jit_solution(10743912029277177495)
XLA Ops:
  9.4 17.5 fusion.273
  26.9 16.7 copy.142
  47.6 8.3 slice.311
  70.7 461.5 %while.4 = (s32[]{:T(128)}, bf16[64,128,2,64]{3,2,1,0:T(2,128)(2,1)}, s32[64,4]{0,1:T(4,128)S(1)}, bf16[64,1,2,64]{3,2,1,0:T(2,128)(2,1)S(1)}, s32[]{:T(128)}, /*index=5*/s32[4]{0:T(128)S(1)}) while((s32[]{:T(128)}, bf16[64,128,2,64]{3,2,1,0:T(2,128)(2,1)}, s32[64,4]{0,1:T(4,128)S(1)}, bf16[64,1,2,64]{3,2,1,0:T(2,128)(2,1)S(1)}, s32[]{:T(128)}, ...), condition=%wide.while_cond, body=%wide.while_body.sunk | while | flops 157 | bytes 3498 | solution.py:107
  532.2 8.8 copy.117
  552.3 9.5 copy.144
  561.8 442.6 %while.5 = (s32[]{:T(128)}, bf16[64,128,2,64]{3,2,1,0:T(2,128)(2,1)}, s32[64,4]{0,1:T(4,128)S(1)}, bf16[64,1,2,64]{3,2,1,0:T(2,128)(2,1)S(1)}, s32[]{:T(128)}, /*index=5*/s32[4]{0:T(128)S(1)}) while((s32[]{:T(128)}, bf16[64,128,2,64]{3,2,1,0:T(2,128)(2,1)}, s32[64,4]{0,1:T(4,128)S(1)}, bf16[64,1,2,64]{3,2,1,0:T(2,128)(2,1)S(1)}, s32[]{:T(128)}, ...), condition=%wide.while_cond.1, body=%wide.while_body.1.sunk | while | flops 157 | bytes 3498 | solution.py:107
  1004.5 8.8 copy.120
  1015.3 9.5 fusion.274
  1025.5 24.9 all-reduce.15
  1050.5 44.5 %fusion.270 = (bf16[1,2048,8192]{2,1,0:T(8,128)(2,1)}, bf16[1,2048,8192]{2,1,0:T(8,128)(2,1)}) fusion(bf16[2,2048,8192]{2,1,0:T(8,128)(2,1)} %param.19), kind=kLoop, calls=%fused_computation.351 | loop fusion | bytes 134217728 | tf_op jit(solution)/shard_map/slice | solution.py:57
  1100.0 44.5 %fusion.271 = (bf16[1,2048,8192]{2,1,0:T(8,128)(2,1)}, bf16[1,2048,8192]{2,1,0:T(8,128)(2,1)}) fusion(bf16[2,2048,8192]{2,1,0:T(8,128)(2,1)} %param.20), kind=kLoop, calls=%fused_computation.352 | loop fusion | bytes 134217728 | tf_op jit(solution)/shard_map/slice | solution.py:58
  1144.6 45.1 %fusion.272 = (bf16[1,8192,2048]{2,1,0:T(8,128)(2,1)}, bf16[1,8192,2048]{2,1,0:T(8,128)(2,1)}) fusion(bf16[2,8192,2048]{2,1,0:T(8,128)(2,1)} %param.21), kind=kLoop, calls=%fused_computation.353 | loop fusion | bytes 134217728 | tf_op jit(solution)/shard_map/slice | solution.py:59
  1189.7 8.9 fusion.124
  1198.5 16.8 copy.145
  1215.3 20.0 all-reduce.16
  1262.9 14.1 conditional.1
  1277.0 451.4 %while.7 = (s32[]{:T(128)}, bf16[64,128,2,64]{3,2,1,0:T(2,128)(2,1)}, s32[64,4]{0,1:T(4,128)S(1)}, bf16[64,1,2,64]{3,2,1,0:T(2,128)(2,1)}, s32[]{:T(128)}, /*index=5*/s32[4]{0:T(128)S(1)}) while((s32[]{:T(128)}, bf16[64,128,2,64]{3,2,1,0:T(2,128)(2,1)}, s32[64,4]{0,1:T(4,128)S(1)}, bf16[64,1,2,64]{3,2,1,0:T(2,128)(2,1)}, s32[]{:T(128)}, ...), condition=%wide.while_cond.3, body=%wide.while_body.3.sunk | while | flops 157 | bytes 3754 | solution.py:107
  1737.7 1253.3 %all-to-all-start = ((bf16[8,256,2048]{2,1,0:T(8,128)(2,1)}), bf16[8,256,2048]{2,1,0:T(8,128)(2,1)}, u32[]{:S(2)}, u32[]{:S(2)}) async-start(bf16[8,256,2048]{2,1,0:T(8,128)(2,1)} %bitcast.46), calls=%async_computation | async-start | bytes 16777216 | tf_op jit(solution)/shard_map/all_to_all | solution.py:188
  2991.7 438.5 %while.6 = (s32[]{:T(128)}, bf16[64,128,2,64]{3,2,1,0:T(2,128)(2,1)}, s32[64,4]{0,1:T(4,128)S(1)}, bf16[64,1,2,64]{3,2,1,0:T(2,128)(2,1)S(1)}, s32[]{:T(128)}, /*index=5*/s32[4]{0:T(128)S(1)}) while((s32[]{:T(128)}, bf16[64,128,2,64]{3,2,1,0:T(2,128)(2,1)}, s32[64,4]{0,1:T(4,128)S(1)}, bf16[64,1,2,64]{3,2,1,0:T(2,128)(2,1)S(1)}, s32[]{:T(128)}, ...), condition=%wide.while_cond.2, body=%wide.while_body.2.sunk | while | flops 157 | bytes 3498 | solution.py:107
  3430.2 8.3 slice.318
  3438.5 9.1 copy.127
  3447.6 8.8 copy.124
  3482.3 9.2 concatenate.131
  3498.7 11.1 gather_fusion
  3509.8 9.2 gather_fusion.1
  3518.9 11.8 broadcast_select_fusion.4
  3530.8 10.5 copy.129
  3546.2 22.6 all-reduce.17
  3574.0 8.9 fusion.118
  3587.7 10.5 copy.131
  3607.3 20.0 all-reduce.18
  (1176 shorter events, 1940.7 us)
Async XLA Ops:
  7.2 1240.8 %all-gather.4.cloned.1.call-start = ((), (), s32[]{:S(2)}) async-start(), calls=%async_computation.3 | async-start | bytes 9437184 | tf_op jit(solution)/shard_map/all_gather | solution.py:161
  8.0 3459.2 %all-gather.6.cloned.1.call-start = ((), (), s32[]{:S(2)}) async-start(), calls=%async_computation.4 | async-start | bytes 5242880 | tf_op jit(solution)/shard_map/all_gather | solution.py:182
  47.6 8.3 copy-start.10
  57.2 13.4 copy-start.43
  57.2 13.5 copy-start.31
  70.1 474.5 %copy-start.41 = (s32[1,64]{1,0:T(1,128)S(1)}, s32[1,64]{1,0:T(1,128)}, u32[]{:S(2)}) copy-start(s32[1,64]{1,0:T(1,128)} %param.25) | copy-start | bytes 772
  70.3 475.1 %copy-start.23 = (f32[64,32]{1,0:T(8,128)}, f32[64,32]{1,0:T(8,128)S(1)}, u32[]{:S(2)}) copy-start(f32[64,32]{1,0:T(8,128)S(1)} %get-tuple-element.288) | copy-start | bytes 24580
  70.3 475.1 %copy-start.25 = (f32[64,32]{1,0:T(8,128)}, f32[64,32]{1,0:T(8,128)S(1)}, u32[]{:S(2)}) copy-start(f32[64,32]{1,0:T(8,128)S(1)} %get-tuple-element.289) | copy-start | bytes 24580
  541.0 11.4 copy-start.4
  544.6 17.2 copy-start.34
  1004.5 20.3 copy-start.21
  1004.5 20.3 copy-start.32
  1013.3 11.5 copy-start.7
  1215.3 25.0 copy-start.9
  1235.5 12.2 copy-start.38
  1247.9 7.0 copy-start.39
  1262.8 14.2 copy-start.22
  1262.8 14.2 copy-start.33
  1262.8 465.6 %copy-start.12 = (bf16[64,2048]{1,0:T(8,128)(2,1)S(1)}, bf16[64,2048]{1,0:T(8,128)(2,1)}, u32[]{:S(2)}) copy-start(bf16[64,2048]{1,0:T(8,128)(2,1)} %copy-done.11) | copy-start | bytes 786436
  1262.9 465.6 %copy-start.37 = (f32[64]{0:T(128)S(1)}, f32[64]{0:T(128)}, u32[]{:S(2)}) copy-start(f32[64]{0:T(128)} %copy-done.36) | copy-start | bytes 772
  1262.9 467.1 %copy-start.8 = (bf16[1,1,64,128,2,64]{3,5,4,2,1,0:T(8,128)(2,1)S(1)}, bf16[1,1,64,128,2,64]{3,5,4,2,1,0:T(8,128)(2,1)}, u32[]{:S(2)}) copy-start(bf16[1,1,64,128,2,64]{3,5,4,2,1,0:T(8,128)(2,1)} %get-tuple-element.274) | copy-start | bytes 6291460
  1276.9 460.4 %copy-start.24 = (f32[64,32]{1,0:T(8,128)S(1)}, f32[64,32]{1,0:T(8,128)}, u32[]{:S(2)}) copy-start(f32[64,32]{1,0:T(8,128)} %copy-done.23) | copy-start | bytes 24580
  1276.9 460.4 %copy-start.26 = (f32[64,32]{1,0:T(8,128)S(1)}, f32[64,32]{1,0:T(8,128)}, u32[]{:S(2)}) copy-start(f32[64,32]{1,0:T(8,128)} %copy-done.25) | copy-start | bytes 24580
  1737.7 1803.7 %all-to-all-start = ((bf16[8,256,2048]{2,1,0:T(8,128)(2,1)}), bf16[8,256,2048]{2,1,0:T(8,128)(2,1)}, u32[]{:S(2)}, u32[]{:S(2)}) async-start(bf16[8,256,2048]{2,1,0:T(8,128)(2,1)} %bitcast.46), calls=%async_computation | async-start | bytes 16777216 | tf_op jit(solution)/shard_map/all_to_all | solution.py:188
  2991.0 483.1 %all-gather.8.cloned.1.call-start = ((), (), s32[]{:S(2)}) async-start(), calls=%async_computation.5 | async-start | bytes 5242880 | tf_op jit(solution)/shard_map/all_gather | solution.py:183
  3447.6 12.4 copy-start.35
  3456.4 10.0 copy-start.6
  3459.7 7.2 copy-start.40
  3459.7 7.3 copy-start.42
  3541.3 56.9 %all-to-all-start.1 = ((bf16[8,2,448,2,64]{2,4,3,1,0:T(8,128)(2,1)}), bf16[8,2,448,2,64]{2,4,3,1,0:T(8,128)(2,1)}, u32[]{:S(2)}, u32[]{:S(2)}) async-start(bf16[8,2,448,2,64]{2,4,3,1,0:T(8,128)(2,1)} %copy.129), calls=%async_computation.1 | async-start | bytes 4194304 | tf_op jit(solution)/shard_map/all_to_all | solution.py:186
  3582.9 20.4 copy-start.5
  3598.3 33.8 all-to-all-start.2
  (2 other events, 7.5 us)
Sparse Core Ops, SparseCore 0:
  9.6 49.2 all-gather.3
  1277.1 1291.5 all-gather.5
  2993.3 46.0 all-gather.7
where the time goes:
time: 3670 us; the launch traced here: 3640 us
  other arithmetic  1660 us (45%)
  starting transfers between devices  1260 us (34%)
  local copies, waits for them, and re-layouts  564 us (15%)
  blocking collectives  87.5 us (2%)
  matrix products  39.3 us (1%)
    scatter x512, other arithmetic  1640 us
    all_to_all x1, starting transfers between devices, local_step(): lax.all_to_all(hidden.reshape(side_size, prompt_rows, model_dim), 'side',...  1250 us
    scatter x512, local copies, waits for them, and re-layouts  158 us
    unnamed x65, local copies, waits for them, and re-layouts  75.8 us
  transfers between devices with their start and end apart: 6, of which 0 were waited for; matrix products, arithmetic and copies ran while one was open for 62% of the time, Pallas kernels for 0%

commit v1 on v0

v1 whole, which is shorter than its diff:
```python
import functools

import jax
import jax.numpy as jnp
from jax import lax
from jax.experimental import pallas as pl
from jax.experimental.pallas import tpu as pltpu
from jax.sharding import PartitionSpec as P

ROPE_BASE = 10000.0
NORM_EPS = 1e-5
BF16 = jnp.bfloat16
F32 = jnp.float32
TILE = 512
W_SLOTS = 10
D_SLOTS = 4
ANY = pl.BlockSpec(memory_space=pl.ANY)
VMEM = pl.BlockSpec(memory_space=pltpu.VMEM)
SMEM = pl.BlockSpec(memory_space=pltpu.SMEM)
NT = (((1,), (1,)), ((), ()))


def rms(wide):
    return (wide * lax.rsqrt(jnp.mean(wide * wide, axis=-1, keepdims=True) + NORM_EPS)).astype(BF16)


def rope_tile(vals, cos, sin):
    wide = vals.astype(F32)
    width = wide.shape[1]
    lane = lax.broadcasted_iota(jnp.int32, wide.shape, 1)
    half = 32
    other = jnp.where(lax.rem(lane, 2 * half) < half, pltpu.roll(wide, width - half, 1), pltpu.roll(wide, half, 1))
    reps = width // cos.shape[1]
    return (wide * jnp.concatenate([cos] * reps, axis=1) + other * jnp.concatenate([sin] * reps, axis=1)).astype(BF16)


def trunk_kernel(layer, has_mid, has_qkv, *refs):
    refs = list(refs)
    h_ref = refs.pop(0)
    if has_mid:
        ctx_ref, wo_ref, wg_ref, wu_ref, wd_ref = refs[:5]
        refs = refs[5:]
    if has_qkv:
        cos_ref, sin_ref, wq_ref = refs[:3]
        refs = refs[3:]
    if has_mid:
        hout_ref = refs.pop(0)
    if has_qkv:
        qkv_ref = refs.pop(0)
    wbuf, wsem, dbuf, dsem, norm_ref, mid_ref, acc_ref = refs

    model = h_ref.shape[1]
    n_out = model // TILE if has_mid else 0
    n_ff = wg_ref.shape[2] // TILE if has_mid else 0
    n_qkv = wq_ref.shape[2] // TILE if has_qkv else 0
    qkv_layer = layer + 1 if has_mid else layer
    first_qkv = n_out + 2 * n_ff
    total = first_qkv + n_qkv

    def cols(src, lay, tile):
        return src.at[lay, :, pl.ds(pl.multiple_of(tile * TILE, TILE), TILE)]

    def w_start(src, lay, tile, slot):
        pltpu.make_async_copy(cols(src, lay, tile), wbuf.at[slot], wsem.at[slot]).start()

    def w_start_static(idx):
        slot = idx % W_SLOTS
        if idx < n_out:
            w_start(wo_ref, layer, idx, slot)
        elif idx < first_qkv:
            w_start((wg_ref, wu_ref)[(idx - n_out) % 2], layer, (idx - n_out) // 2, slot)
        elif idx < total:
            w_start(wq_ref, qkv_layer, idx - first_qkv, slot)

    def w_wait(slot):
        src = wq_ref if has_qkv else wo_ref
        pltpu.make_async_copy(cols(src, 0, 0), wbuf.at[slot], wsem.at[slot]).wait()

    def d_copy(chunk, slot):
        return pltpu.make_async_copy(wd_ref.at[layer, pl.ds(pl.multiple_of(chunk * TILE, TILE), TILE), :], dbuf.at[slot], dsem.at[slot])

    for idx in range(min(W_SLOTS, total)):
        w_start_static(idx)
        if has_mid and n_out <= idx < n_out + D_SLOTS:
            d_copy(idx - n_out, idx - n_out).start()

    if has_mid:
        for tile in range(n_out):
            slot = tile % W_SLOTS
            w_wait(slot)
            sl = slice(tile * TILE, (tile + 1) * TILE)
            out = jnp.dot(ctx_ref[...], wbuf[slot], preferred_element_type=F32).astype(BF16)
            w_start_static(tile + W_SLOTS)
            mid_ref[:, sl] = h_ref[:, sl].astype(F32) + out.astype(F32)
        hidden = mid_ref[...].astype(BF16)
        mid_ref[...] = hidden.astype(F32)
        norm_ref[...] = rms(mid_ref[...])
        acc_ref[...] = jnp.zeros_like(acc_ref)

        def chunk_step(chunk, carry):
            base = n_out + 2 * chunk
            slot_g = lax.rem(base, W_SLOTS)
            slot_u = lax.rem(base + 1, W_SLOTS)
            slot_d = lax.rem(chunk, D_SLOTS)
            w_wait(slot_g)
            gate = jnp.dot(norm_ref[...], wbuf[slot_g], preferred_element_type=F32).astype(BF16).astype(F32)
            w_wait(slot_u)
            upper = jnp.dot(norm_ref[...], wbuf[slot_u], preferred_element_type=F32).astype(BF16).astype(F32)
            act = (jax.nn.silu(gate) * upper).astype(BF16)
            ahead = W_SLOTS // 2

            @pl.when(chunk + ahead < n_ff)
            def _():
                w_start(wg_ref, layer, chunk + ahead, slot_g)
                w_start(wu_ref, layer, chunk + ahead, slot_u)

            if has_qkv:
                later = 2 * (chunk + ahead - n_ff)

                @pl.when((chunk + ahead >= n_ff) & (later < n_qkv))
                def _():
                    w_start(wq_ref, qkv_layer, later, slot_g)
                    w_start(wq_ref, qkv_layer, later + 1, slot_u)

            d_copy(chunk, slot_d).wait()
            acc_ref[...] += jnp.dot(act, dbuf[slot_d], preferred_element_type=F32)

            @pl.when(chunk + D_SLOTS < n_ff)
            def _():
                d_copy(chunk + D_SLOTS, slot_d).start()

            return carry

        lax.fori_loop(0, n_ff, chunk_step, 0)
        hidden = (mid_ref[...] + acc_ref[...].astype(BF16).astype(F32)).astype(BF16)
        hout_ref[...] = hidden
    else:
        hidden = h_ref[...]
    if has_qkv:
        norm_ref[...] = rms(hidden.astype(F32))
        for tile in range(n_qkv):
            slot = (first_qkv + tile) % W_SLOTS
            w_wait(slot)
            sl = slice(tile * TILE, (tile + 1) * TILE)
            out = jnp.dot(norm_ref[...], wbuf[slot], preferred_element_type=F32).astype(BF16)
            if (first_qkv + tile + W_SLOTS) < total and not has_mid:
                w_start_static(first_qkv + tile + W_SLOTS)
            if tile < n_qkv - 1:
                out = rope_tile(out, cos_ref[...], sin_ref[...])
            qkv_ref[:, sl] = out


def trunk(layer, hidden, ctx, cos, sin, w_qkv, w_out, w_gate, w_up, w_down):
    rows, model = hidden.shape
    has_mid = ctx is not None
    has_qkv = cos is not None
    args, specs, outs = [hidden], [VMEM], []
    if has_mid:
        args += [ctx, w_out, w_gate, w_up, w_down]
        specs += [VMEM, ANY, ANY, ANY, ANY]
        outs.append(jax.ShapeDtypeStruct((rows, model), BF16))
    if has_qkv:
        args += [cos, sin, w_qkv]
        specs += [VMEM, VMEM, ANY]
        outs.append(jax.ShapeDtypeStruct((rows, w_qkv.shape[2]), BF16))
    return pl.pallas_call(
        functools.partial(trunk_kernel, layer, has_mid, has_qkv),
        out_shape=outs,
        in_specs=specs,
        out_specs=[VMEM] * len(outs),
        scratch_shapes=[
            pltpu.VMEM((W_SLOTS, model, TILE), BF16),
            pltpu.SemaphoreType.DMA((W_SLOTS,)),
            pltpu.VMEM((D_SLOTS, TILE, model), BF16),
            pltpu.SemaphoreType.DMA((D_SLOTS,)),
            pltpu.VMEM((rows, model), BF16),
            pltpu.VMEM((rows, model), F32),
            pltpu.VMEM((rows, model), F32),
        ],
        compiler_params=pltpu.CompilerParams(vmem_limit_bytes=48 * 2**20),
        name="trunk",
    )(*args)


def prompt_attn_kernel(head_dim, rep, start_ref, seg_ref, q_ref, kv_hbm, out_ref, kv_ref, sem):
    window = kv_ref.shape[0]
    kv_cols = kv_ref.shape[1] // 2
    rows = q_ref.shape[0]
    key0 = pl.multiple_of(start_ref[0], 16)
    copy = pltpu.make_async_copy(kv_hbm.at[pl.ds(key0, window), :], kv_ref, sem)
    copy.start()
    key_row = key0 + lax.broadcasted_iota(jnp.int32, (rows, window), 1)
    q_row = start_ref[1] + lax.broadcasted_iota(jnp.int32, (rows, window), 0)
    allowed = (key_row <= q_row) & (key_row >= seg_ref[...])
    scale = head_dim ** -0.5
    copy.wait()
    for head in range(kv_cols // head_dim):
        k_head = kv_ref[:, head * head_dim:(head + 1) * head_dim]
        v_head = kv_ref[:, kv_cols + head * head_dim:kv_cols + (head + 1) * head_dim]
        outs = []
        for sub in range(rep):
            at = (head * rep + sub) * head_dim
            scores = lax.dot_general(q_ref[:, at:at + head_dim], k_head, NT, preferred_element_type=F32) * scale
            scores = jnp.where(allowed, scores, -1e30)
            scores = jnp.exp(scores - jnp.max(scores, axis=-1, keepdims=True))
            prob = (scores * (1.0 / jnp.sum(scores, axis=-1, keepdims=True))).astype(BF16)
            outs.append(jnp.dot(prob, v_head, preferred_element_type=F32).astype(BF16))
        out_ref[:, head * rep * head_dim:(head + 1) * rep * head_dim] = jnp.concatenate(outs, axis=1)


def prompt_attn(query, kv_all, key0, row0, seg_start, window, head_dim, rep):
    rows = query.shape[0]
    return pl.pallas_call(
        functools.partial(prompt_attn_kernel, head_dim, rep),
        out_shape=jax.ShapeDtypeStruct(query.shape, BF16),
        in_specs=[SMEM, VMEM, VMEM, ANY],
        out_specs=VMEM,
        scratch_shapes=[pltpu.VMEM((window, kv_all.shape[1]), BF16), pltpu.SemaphoreType.DMA],
        compiler_params=pltpu.CompilerParams(vmem_limit_bytes=32 * 2**20),
        name="prompt_attn",
    )(jnp.stack([key0, row0]).astype(jnp.int32), seg_start, query, kv_all)


def decode_attn_kernel(head_dim, rep, pairs_per_b, len_ref, lenrow_ref, q_ref, kn_ref, vn_ref, k_ref, v_ref, *rest):
    ctx_ref, kout_ref, vout_ref = rest[-3:]
    step = pl.program_id(0)
    t_len = k_ref.shape[1]
    pairs = k_ref.shape[0] // head_dim
    group = 4
    batch = pairs // pairs_per_b
    t_iota = lax.broadcasted_iota(jnp.int32, (head_dim, t_len), 1)
    for pair in range(pairs):
        at = len_ref[step * batch + pair // pairs_per_b]
        here = t_iota == at
        sl = slice(pair * head_dim, (pair + 1) * head_dim)
        kout_ref[sl, :] = jnp.where(here, kn_ref[:, pair:pair + 1].astype(F32), k_ref[sl, :].astype(F32)).astype(BF16)
        vout_ref[sl, :] = jnp.where(here, vn_ref[:, pair:pair + 1].astype(F32), v_ref[sl, :].astype(F32)).astype(BF16)
    rows = group * rep
    width = group * head_dim
    diag = (lax.broadcasted_iota(jnp.int32, (rows, width), 0) // rep) == (lax.broadcasted_iota(jnp.int32, (rows, width), 1) // head_dim)
    scores = []
    for g in range(pairs // group):
        q_part = q_ref[g * rows:(g + 1) * rows, :].astype(F32)
        lhs = jnp.where(diag, jnp.concatenate([q_part] * group, axis=1), 0.0).astype(BF16)
        scores.append(jnp.dot(lhs, kout_ref[g * width:(g + 1) * width, :], preferred_element_type=F32))
    scores = jnp.concatenate(scores, axis=0) * (head_dim ** -0.5)
    t_row = lax.broadcasted_iota(jnp.int32, scores.shape, 1)
    scores = jnp.where(t_row <= lenrow_ref[...], scores, -1e30)
    scores = jnp.exp(scores - jnp.max(scores, axis=-1, keepdims=True))
    prob = (scores * (1.0 / jnp.sum(scores, axis=-1, keepdims=True))).astype(BF16)
    fold = (lax.rem(lax.broadcasted_iota(jnp.int32, (width, head_dim), 0), head_dim) == lax.broadcasted_iota(jnp.int32, (width, head_dim), 1)).astype(F32).astype(BF16)
    for g in range(pairs // group):
        full = lax.dot_general(prob[g * rows:(g + 1) * rows, :], vout_ref[g * width:(g + 1) * width, :], NT, preferred_element_type=F32)
        own = jnp.where(diag, full, 0.0).astype(BF16)
        ctx_ref[g * rows:(g + 1) * rows, :] = jnp.dot(own, fold, preferred_element_type=F32).astype(BF16)


def decode_attn(layer, query, k_cols, v_cols, lengths, kc, vc, prev, head_dim, rep, pairs_per_b, steps):
    layers, depth, t_len = kc.shape
    block = depth // steps
    q_rows = query.shape[0] // steps
    len_rows = jnp.repeat(lengths, pairs_per_b * rep)[:, None]
    cache_in = pl.BlockSpec((None, block, t_len), lambda i: (layer, i, 0))
    col_in = pl.BlockSpec((None, head_dim, k_cols.shape[2]), lambda i: (i, 0, 0))
    row_in = pl.BlockSpec((q_rows, head_dim), lambda i: (i, 0))
    args = [lengths, len_rows, query, k_cols, v_cols, kc, vc]
    specs = [SMEM, pl.BlockSpec((q_rows, 1), lambda i: (i, 0)), row_in, col_in, col_in, cache_in, cache_in]
    aliases = {}
    if prev is not None:
        args += list(prev)
        specs += [ANY, ANY]
        aliases = {7: 1, 8: 2}
    return pl.pallas_call(
        functools.partial(decode_attn_kernel, head_dim, rep, pairs_per_b),
        out_shape=[jax.ShapeDtypeStruct(query.shape, BF16), jax.ShapeDtypeStruct(kc.shape, BF16), jax.ShapeDtypeStruct(vc.shape, BF16)],
        grid=(steps,),
        in_specs=specs,
        out_specs=[row_in, cache_in, cache_in],
        input_output_aliases=aliases,
        compiler_params=pltpu.CompilerParams(vmem_limit_bytes=32 * 2**20),
        name="decode_attn",
    )(*args)


def solution(mesh):
    tp = mesh.shape['tp']
    side = mesh.shape['side']
    rows_spec = P(('pair', 'side'), None)
    batch_spec = P(('pair', 'side'), None, None)
    cache_spec = P(('pair', 'side'), None, None, None, 'tp', None)
    prompt_spec = P(('pair', 'side'), None, None, 'tp', None)

    def local_step(x_loc, req_len, dest, w_qkv, w_out, w_gate, w_up, w_down, y_loc, kc_loc, vc_loc, clen_loc):
        s_idx = lax.axis_index('side')
        t_idx = lax.axis_index('tp')
        layers = w_qkv.shape[0]
        head_dim = kc_loc.shape[-1]
        slots = kc_loc.shape[-2]
        t_len = kc_loc.shape[3]
        batch = y_loc.shape[1]
        kv_heads = slots * tp
        rep = w_out.shape[1] // head_dim // kv_heads
        q_cols = w_out.shape[1]
        kv_cols = kv_heads * head_dim
        prompt_rows = x_loc.shape[0]
        seq_len = prompt_rows * side
        max_req = 2 * prompt_rows - prompt_rows // 4
        p_rows = prompt_rows // tp
        d_rows = batch // tp

        hidden = jnp.concatenate([lax.dynamic_slice_in_dim(x_loc, t_idx * p_rows, p_rows, 0), lax.dynamic_slice_in_dim(y_loc[0], t_idx * d_rows, d_rows, 0)], axis=0)
        row0 = s_idx * prompt_rows + t_idx * p_rows
        ids = jnp.arange(side)
        ends = jnp.sum(jnp.where(ids[None, :] <= ids[:, None], req_len[None, :], 0), axis=1)
        row_ids = row0 + jnp.arange(p_rows)
        seg_start = jnp.sum(jnp.where(row_ids[:, None] >= ends[None, :], req_len[None, :], 0), axis=1)
        lengths = clen_loc[0]
        positions = jnp.concatenate([row_ids - seg_start, lax.dynamic_slice_in_dim(lengths, t_idx * d_rows, d_rows, 0)])
        half = head_dim // 2
        inv_freq = ROPE_BASE ** (-jnp.arange(half, dtype=F32) / half)
        angles = positions.astype(F32)[:, None] * inv_freq
        cos = jnp.cos(angles)
        sin = jnp.sin(angles)
        cos = jnp.concatenate([cos] * 4, axis=1)
        sin = jnp.concatenate([-sin, sin] * 2, axis=1)
        window = -(-(max_req - 1) // p_rows) * p_rows + p_rows
        key0 = jnp.maximum(row0 + p_rows - window, 0)

        kc = jnp.transpose(kc_loc[0], (0, 1, 3, 4, 2)).reshape(layers, batch * slots * head_dim, t_len)
        vc = jnp.transpose(vc_loc[0], (0, 1, 3, 4, 2)).reshape(layers, batch * slots * head_dim, t_len)
        steps = 8
        group_w = rep * head_dim

        (qkv,) = trunk(0, hidden, None, cos, sin, w_qkv, w_out, w_gate, w_up, w_down)
        caches = None
        kv_layers = []
        for layer in range(layers):
            kv_all = lax.all_gather(qkv[:p_rows, q_cols:], ('side', 'tp'), axis=0, tiled=True)
            kv_layers.append(kv_all)
            dec = qkv[p_rows:]
            dec_q = dec[:, :q_cols].reshape(d_rows, slots, tp, group_w)
            dec_k = dec[:, q_cols:q_cols + kv_cols].reshape(d_rows, slots, tp, head_dim)
            dec_v = dec[:, q_cols + kv_cols:].reshape(d_rows, slots, tp, head_dim)
            send = jnp.transpose(jnp.concatenate([dec_q, dec_k, dec_v], axis=3), (2, 0, 1, 3))
            got = lax.all_to_all(send, 'tp', 0, 0, tiled=True).reshape(batch, slots, group_w + 2 * head_dim)
            q_dec = got[:, :, :group_w].reshape(batch * slots * rep, head_dim)
            k_new = jnp.transpose(got[:, :, group_w:group_w + head_dim].reshape(steps, batch * slots // steps, head_dim), (0, 2, 1))
            v_new = jnp.transpose(got[:, :, group_w + head_dim:].reshape(steps, batch * slots // steps, head_dim), (0, 2, 1))
            ctx_p = prompt_attn(qkv[:p_rows, :q_cols], kv_all, key0, row0, seg_start[:, None].astype(jnp.int32), window, head_dim, rep)
            ctx_d, k_out, v_out = decode_attn(layer, q_dec, k_new, v_new, lengths, kc, vc, caches, head_dim, rep, slots, steps)
            caches = (k_out, v_out)
            back = lax.all_to_all(ctx_d.reshape(tp, d_rows, slots, group_w), 'tp', 0, 0, tiled=True)
            ctx = jnp.concatenate([ctx_p, jnp.transpose(back, (1, 2, 0, 3)).reshape(d_rows, q_cols)], axis=0)
            if layer + 1 < layers:
                hidden, qkv = trunk(layer, hidden, ctx, cos, sin, w_qkv, w_out, w_gate, w_up, w_down)
            else:
                (hidden,) = trunk(layer, hidden, ctx, None, None, w_qkv, w_out, w_gate, w_up, w_down)
        all_hidden = lax.all_gather(hidden, 'tp', axis=0)
        hidden_rows = all_hidden[:, :p_rows].reshape(prompt_rows, -1)
        dec_out = all_hidden[:, p_rows:].reshape(batch, -1)

        mine = dest == s_idx
        starts = ends - req_len
        start = jnp.sum(jnp.where(mine, starts, 0))
        length = jnp.sum(jnp.where(mine, req_len, 0))
        keep = (jnp.arange(max_req) < length)[None, :, None, None, None]
        full = jnp.stack(kv_layers).reshape(layers, seq_len, 2, slots, tp, head_dim)
        full = lax.dynamic_index_in_dim(full, t_idx, axis=4, keepdims=False)
        full = jnp.concatenate([full, jnp.zeros((layers, max_req) + full.shape[2:], BF16)], axis=1)
        piece = lax.dynamic_slice_in_dim(full, start, max_req, axis=1)
        piece = jnp.where(keep, piece, jnp.zeros_like(piece))

        def cache_back(arr):
            return jnp.transpose(arr.reshape(layers, batch, slots, head_dim, t_len), (0, 1, 4, 2, 3))[None]

        return hidden_rows, dec_out[None], piece[:, :, 0][None], piece[:, :, 1][None], cache_back(caches[0]), cache_back(caches[1])

    return jax.shard_map(local_step, mesh=mesh,
                         in_specs=(rows_spec, P('pair'), P('pair'), P(), P(), P(), P(), P(), batch_spec, cache_spec, cache_spec, rows_spec),
                         out_specs=(rows_spec, batch_spec, prompt_spec, prompt_spec, cache_spec, cache_spec),
                         check_vma=False)
```

time: 3670 us -> 238 us (0.06)
  other arithmetic: 1660 us -> 6.54 us
  starting transfers between devices: 1260 us -> 13.3 us
  local copies, waits for them, and re-layouts: 564 us -> 37.8 us
  Pallas kernels: 0 us -> 123 us
  blocking collectives: 87.5 us -> 8.46 us
  matrix products: 39.3 us -> 0 us
    scatter x513 -> x0, other arithmetic: 1640 us -> none
    all_to_all x3, starting transfers between devices: 1260 us -> 12.7 us  [the longest x2 6.75 us: local_step(): lax.all_to_all(ctx_d.reshape(tp, d_rows, slots, group_w), 'tp', 0, 0, til...]
    slice x13 -> x14, local copies, waits for them, and re-layouts: 199 us -> 5.67 us  [the longest x1 2.3 us: local_step(): hidden_rows = all_hidden[:, :p_rows].reshape(prompt_rows, -1)]
    scatter x516 -> x0, local copies, waits for them, and re-layouts: 193 us -> none
    pallas_call x0 -> x7, Pallas kernels: none -> 123 us  [the longest x3 79.1 us: trunk(): pl.pallas_call(functools.partial(trunk_kernel, layer, has_mid, has_qkv),...]
    psum x4 -> x0, blocking collectives: 87.5 us -> none  [the longest x2 47.5 us: finish_layer(): lax.psum(jnp.dot(context, wo_l, preferred_element_type=jnp.float32), 'tp')]
    unnamed x65 -> x22, local copies, waits for them, and re-layouts: 75.8 us -> 13.2 us
    dot_general x16 -> x0, matrix products: 39.3 us -> none  [the longest x2 17.8 us: finish_layer(): jnp.dot(activated, wd_l, preferred_element_type=jnp.float32)]
  transfers between devices with their start and end apart: 6 -> 6, of which waited for: 0 -> 6; matrix products, arithmetic and copies ran while one was open for 62% -> 9% of each run, Pallas kernels for 0% -> 9%
where the time goes in v1:
time: 238 us; the launch traced here: 237 us
  Pallas kernels  123 us (52%)
  local copies, waits for them, and re-layouts  37.8 us (16%)
  waiting for transfers between devices  31.5 us (13%)
  between operations  16.1 us (7%)
  starting transfers between devices  13.3 us (6%)
  blocking collectives  8.46 us (4%)
  other arithmetic  6.54 us (3%)
    pallas_call x3, Pallas kernels, trunk(): pl.pallas_call(functools.partial(trunk_kernel, layer, has_mid, has_qkv),...  79.1 us
    pallas_call x2, Pallas kernels, prompt_attn(): pl.pallas_call(functools.partial(prompt_attn_kernel, head_dim, rep), out_...  23.4 us
    pallas_call x2, Pallas kernels, decode_attn(): pl.pallas_call(functools.partial(decode_attn_kernel, head_dim, rep, pairs...  20.6 us
    unnamed x22, local copies, waits for them, and re-layouts  13.2 us
    all_gather x2, local copies, waits for them, and re-layouts, local_step(): lax.all_gather(qkv[:p_rows, q_cols:], ('side', 'tp'), axis=0, tiled=True)  13.1 us
    all_gather x2, waiting for transfers between devices, local_step(): lax.all_gather(qkv[:p_rows, q_cols:], ('side', 'tp'), axis=0, tiled=True)  11.7 us
    all_to_all x2, waiting for transfers between devices, local_step(): lax.all_to_all(ctx_d.reshape(tp, d_rows, slots, group_w), 'tp', 0, 0, til...  11.3 us
    all_to_all x1, blocking collectives, local_step(): lax.all_to_all(send, 'tp', 0, 0, tiled=True)  8.46 us
  transfers between devices with their start and end apart: 6, of which 6 were waited for; matrix products, arithmetic and copies ran while one was open for 9% of the time, Pallas kernels for 9%

profile of v1, /device:TPU:98, one launch (start us, length us, event | category | flops | bytes accessed | tf_op | source)
XLA Modules:
  0.0 236.8 jit_solution(17685890095338859355)
XLA Ops:
  7.3 0.8 select_reduce_fusion.1
  9.6 0.8 dynamic-slice_bitcast_fusion
  11.0 5.4 %trunk.3 = bf16[80,3072]{1,0:T(8,128)(2,1)S(1)} custom-call(bf16[80,2048]{1,0:T(8,128)(2,1)S(1)} %pad_maximum_fusion.refs_0_, f32[80,128]{1,0:T(8,128)S(1)} %get-tuple-element.37.refs_1_.refs_6_, f32[80,128]{1,0:T(8,128)S(1)} %get-tuple-element.38.refs_2_.refs_7_, bf16[2,2048,3072]{2,1,0:T(8,128)(2,1)} %refs_8_.1), custom_call_target="tpu_custom_call" | custom-call | tf_op jit(solution)/shard_map/trunk/pallas_call | solution.py:166
  17.5 0.8 maximum_bitcast_fusion
  18.3 5.9 %all-to-all-start = ((bf16[4,16,2,384]{3,2,1,0:T(2,128)(2,1)}), bf16[4,16,2,384]{3,2,1,0:T(2,128)(2,1)S(1)}, u32[]{:S(2)}, u32[]{:S(2)}) async-start(bf16[4,16,2,384]{3,2,1,0:T(2,128)(2,1)} %maximum_bitcast_fusion), calls=%async_computation | async-start | bytes 196608 | tf_op jit(solution)/shard_map/all_to_all | solution.py:345
  24.4 5.4 %all-to-all-done = bf16[4,16,2,384]{3,2,1,0:T(2,128)(2,1)S(1)} async-done(((bf16[4,16,2,384]{3,2,1,0:T(2,128)(2,1)}), bf16[4,16,2,384]{3,2,1,0:T(2,128)(2,1)S(1)}, u32[]{:S(2)}, u32[]{:S(2)}) %all-to-all-start) | async-done | bytes 98336 | tf_op jit(solution)/shard_map/all_to_all | solution.py:345
  30.4 2.2 copy-done.2
  32.6 2.2 copy-done.4
  34.8 10.3 %decode_attn.2 = (bf16[512,64]{1,0:T(8,128)(2,1)S(1)}, bf16[2,8192,128]{2,1,0:T(8,128)(2,1)}, bf16[2,8192,128]{2,1,0:T(8,128)(2,1)}) custom-call(s32[64]{0:T(128)S(1)} %bitcast.64, s32[512,1]{1,0:T(8,128)S(1)} %broadcast_in_dim_reshape.9.lenrow_ref, bf16[512,64]{1,0:T(8,128)(2,1)S(1)} %reshape.124.q_ref, bf16[8,64,16]{2,1,0:T(8,128)(2,1)S(1)} %bitcast.61, ...), custom_call_target="tpu_custom_call" | custom-call | tf_op jit(solution)/shard_map/decode_attn/pallas_call | solution.py:273
  45.8 3.4 %all-to-all-start.1 = ((bf16[4,16,2,256]{3,2,1,0:T(2,128)(2,1)}), bf16[4,16,2,256]{3,2,1,0:T(2,128)(2,1)S(1)}, u32[]{:S(2)}, u32[]{:S(2)}) async-start(bf16[4,16,2,256]{3,2,1,0:T(2,128)(2,1)} %reshape.129), calls=%async_computation.1 | async-start | bytes 131072 | tf_op jit(solution)/shard_map/all_to_all | solution.py:352
  49.7 5.6 %all-to-all-done.1 = bf16[4,16,2,256]{3,2,1,0:T(2,128)(2,1)S(1)} async-done(((bf16[4,16,2,256]{3,2,1,0:T(2,128)(2,1)}), bf16[4,16,2,256]{3,2,1,0:T(2,128)(2,1)S(1)}, u32[]{:S(2)}, u32[]{:S(2)}) %all-to-all-start.1) | async-done | bytes 65568 | tf_op jit(solution)/shard_map/all_to_all | solution.py:352
  55.3 5.7 %all-gather.5.cloned.1.call-done.kv_hbm = bf16[2048,1024]{1,0:T(8,128)(2,1)} async-done(((bf16[64,1024]{1,0:T(8,128)(2,1)}), bf16[2048,1024]{1,0:T(8,128)(2,1)}) %all-gather.5.cloned.1.call-update) | async-done | bytes 4194320 | tf_op jit(solution)/shard_map/all_gather | solution.py:338
  61.0 2.2 copy-done.6
  63.2 11.7 %prompt_attn.2 = bf16[64,2048]{1,0:T(8,128)(2,1)S(1)} custom-call(s32[2]{0:T(128)S(1)} %pad_add_fusion.start_ref, s32[64,1]{1,0:T(8,128)S(1)} %copy.73.seg_ref, bf16[64,2048]{1,0:T(8,128)(2,1)S(1)} %slice.88.q_ref, bf16[2048,1024]{1,0:T(8,128)(2,1)S(1)} %copy-done.6), custom_call_target="tpu_custom_call" | custom-call | tf_op jit(solution)/shard_map/prompt_attn/pallas_call | solution.py:213
  75.0 38.4 %trunk.4 = (bf16[80,2048]{1,0:T(8,128)(2,1)S(1)}, bf16[80,3072]{1,0:T(8,128)(2,1)S(1)}) custom-call(bf16[80,2048]{1,0:T(8,128)(2,1)S(1)} %pad_maximum_fusion.refs_0_, bf16[80,2048]{1,0:T(8,128)(2,1)S(1)} %pad_maximum_fusion.1.refs_1_, bf16[2,2048,2048]{2,1,0:T(8,128)(2,1)} %refs_2_.3, bf16[2,2048,8192]{2,1,0:T(8,128)(2,1)} %refs_3_.5, ...), custom_call_target="tpu_custom_call" | custom-call | tf_op jit(solution)/shard_map/trunk/pallas_call | solution.py:166
  114.7 8.5 %all_to_all.20 = bf16[4,16,2,384]{3,2,1,0:T(2,128)(2,1)S(1)} all-to-all(bf16[4,16,2,384]{3,2,1,0:T(2,128)(2,1)S(1)} %maximum_bitcast_fusion.1), channel_id=1, replica_groups=mesh['pair'=1,'tp'=4,'side'=8] {'tp'}, dimensions={0} | all-to-all | bytes 196608 | tf_op jit(solution)/shard_map/all_to_all | solution.py:345
  123.7 2.2 copy-done.3
  125.9 2.2 copy-done.5
  128.1 10.3 %decode_attn.3 = (bf16[512,64]{1,0:T(8,128)(2,1)S(1)}, bf16[2,8192,128]{2,1,0:T(8,128)(2,1)}, bf16[2,8192,128]{2,1,0:T(8,128)(2,1)}) custom-call(s32[64]{0:T(128)S(1)} %bitcast.65, s32[512,1]{1,0:T(8,128)S(1)} %broadcast_in_dim_reshape.9.lenrow_ref, bf16[512,64]{1,0:T(8,128)(2,1)S(1)} %reshape.135.q_ref, ...), custom_call_target="tpu_custom_call", output_to_operand_aliasing={{1}: (7, {}), {2}: (8, {})} | custom-call | tf_op jit(solution)/shard_map/decode_attn/pallas_call | solution.py:273
  139.2 3.4 %all-to-all-start.3 = ((bf16[4,16,2,256]{3,2,1,0:T(2,128)(2,1)}), bf16[4,16,2,256]{3,2,1,0:T(2,128)(2,1)S(1)}, u32[]{:S(2)}, u32[]{:S(2)}) async-start(bf16[4,16,2,256]{3,2,1,0:T(2,128)(2,1)} %reshape.138), calls=%async_computation.3 | async-start | bytes 131072 | tf_op jit(solution)/shard_map/all_to_all | solution.py:352
  142.9 5.7 %all-to-all-done.3 = bf16[4,16,2,256]{3,2,1,0:T(2,128)(2,1)S(1)} async-done(((bf16[4,16,2,256]{3,2,1,0:T(2,128)(2,1)}), bf16[4,16,2,256]{3,2,1,0:T(2,128)(2,1)S(1)}, u32[]{:S(2)}, u32[]{:S(2)}) %all-to-all-start.3) | async-done | bytes 65568 | tf_op jit(solution)/shard_map/all_to_all | solution.py:352
  148.7 6.0 %all-gather.7.cloned.1.call-done.kv_hbm = bf16[2048,1024]{1,0:T(8,128)(2,1)} async-done(((bf16[64,1024]{1,0:T(8,128)(2,1)}), bf16[2048,1024]{1,0:T(8,128)(2,1)}) %all-gather.7.cloned.1.call-update) | async-done | bytes 4194320 | tf_op jit(solution)/shard_map/all_gather | solution.py:338
  154.7 2.2 copy-done.7
  156.9 11.7 %prompt_attn.3 = bf16[64,2048]{1,0:T(8,128)(2,1)S(1)} custom-call(s32[2]{0:T(128)S(1)} %pad_add_fusion.start_ref, s32[64,1]{1,0:T(8,128)S(1)} %copy.73.seg_ref, bf16[64,2048]{1,0:T(8,128)(2,1)S(1)} %slice.76.q_ref, bf16[2048,1024]{1,0:T(8,128)(2,1)S(1)} %copy-done.7), custom_call_target="tpu_custom_call" | custom-call | tf_op jit(solution)/shard_map/prompt_attn/pallas_call | solution.py:213
  168.7 35.2 %trunk.5 = bf16[80,2048]{1,0:T(8,128)(2,1)} custom-call(bf16[80,2048]{1,0:T(8,128)(2,1)S(1)} %get-tuple-element.15.refs_0_, bf16[80,2048]{1,0:T(8,128)(2,1)S(1)} %pad_maximum_fusion.2.refs_1_, bf16[2,2048,2048]{2,1,0:T(8,128)(2,1)} %refs_2_.3, bf16[2,2048,8192]{2,1,0:T(8,128)(2,1)} %refs_3_.5, bf16[2,2048,8192]{2,1,0:T(8,128)(2,1)} %refs_4_.3, ...), custom_call_target="tpu_custom_call" | custom-call | tf_op jit(solution)/shard_map/trunk/pallas_call | solution.py:166
  207.2 6.5 %copy.89 = bf16[2048,1024]{0,1:T(8,128)(2,1)} copy(bf16[2048,1024]{1,0:T(8,128)(2,1)} %all-gather.5.cloned.1.call-done.kv_hbm) | data formatting | bytes 8388608 | tf_op jit(solution)/shard_map/all_gather | solution.py:338
  213.7 6.6 %copy.90 = bf16[2048,1024]{0,1:T(8,128)(2,1)} copy(bf16[2048,1024]{1,0:T(8,128)(2,1)} %all-gather.7.cloned.1.call-done.kv_hbm) | data formatting | bytes 8388608 | tf_op jit(solution)/shard_map/all_gather | solution.py:338
  220.3 1.8 fusion.1
  222.5 0.8 slice_bitcast_fusion
  223.3 3.0 %all-gather.9.cloned.1.call-done = bf16[320,2048]{1,0:T(8,128)(2,1)} async-done(((bf16[80,2048]{1,0:T(8,128)(2,1)}), bf16[320,2048]{1,0:T(8,128)(2,1)}) %all-gather.9.cloned.1.call-update) | async-done | bytes 1310736 | tf_op jit(solution)/shard_map/all_gather | solution.py:358
  226.3 1.7 slice.100
  228.0 2.3 slice.99
  (78 shorter events, 9.8 us)
Async XLA Ops:
  7.2 3.6 %copy-start = (bf16[256,2048]{1,0:T(8,128)(2,1)S(1)}, bf16[256,2048]{1,0:T(8,128)(2,1)}, u32[]{:S(2)}) copy-start(bf16[256,2048]{1,0:T(8,128)(2,1)} %param.12) | copy-start | bytes 3145732
  7.2 53.8 %all-gather.5.cloned.1.call-start = ((), (), s32[]{:S(2)}) async-start(), calls=%async_computation.4 | async-start | bytes 4325376 | tf_op jit(solution)/shard_map/all_gather | solution.py:338
  11.0 13.3 %copy-start.8 = (s32[1,64]{1,0:T(1,128)S(1)}, s32[1,64]{1,0:T(1,128)}, u32[]{:S(2)}) copy-start(s32[1,64]{1,0:T(1,128)} %param.23) | copy-start | bytes 772
  18.3 11.5 %all-to-all-start = ((bf16[4,16,2,384]{3,2,1,0:T(2,128)(2,1)}), bf16[4,16,2,384]{3,2,1,0:T(2,128)(2,1)S(1)}, u32[]{:S(2)}, u32[]{:S(2)}) async-start(bf16[4,16,2,384]{3,2,1,0:T(2,128)(2,1)} %maximum_bitcast_fusion), calls=%async_computation | async-start | bytes 196608 | tf_op jit(solution)/shard_map/all_to_all | solution.py:345
  30.4 2.2 copy-start.2
  32.6 2.2 copy-start.4
  45.8 9.4 %all-to-all-start.1 = ((bf16[4,16,2,256]{3,2,1,0:T(2,128)(2,1)}), bf16[4,16,2,256]{3,2,1,0:T(2,128)(2,1)S(1)}, u32[]{:S(2)}, u32[]{:S(2)}) async-start(bf16[4,16,2,256]{3,2,1,0:T(2,128)(2,1)} %reshape.129), calls=%async_computation.1 | async-start | bytes 131072 | tf_op jit(solution)/shard_map/all_to_all | solution.py:352
  49.2 105.5 %all-gather.7.cloned.1.call-start = ((), (), s32[]{:S(2)}) async-start(), calls=%async_computation.5 | async-start | bytes 4325376 | tf_op jit(solution)/shard_map/all_gather | solution.py:338
  61.0 2.2 copy-start.6
  123.7 2.2 copy-start.3
  125.9 2.2 copy-start.5
  139.2 9.4 %all-to-all-start.3 = ((bf16[4,16,2,256]{3,2,1,0:T(2,128)(2,1)}), bf16[4,16,2,256]{3,2,1,0:T(2,128)(2,1)S(1)}, u32[]{:S(2)}, u32[]{:S(2)}) async-start(bf16[4,16,2,256]{3,2,1,0:T(2,128)(2,1)} %reshape.138), calls=%async_computation.3 | async-start | bytes 131072 | tf_op jit(solution)/shard_map/all_to_all | solution.py:352
  142.6 83.7 %all-gather.9.cloned.1.call-start = ((), (), s32[]{:S(2)}) async-start(), calls=%async_computation.6 | async-start | bytes 1638400 | tf_op jit(solution)/shard_map/all_gather | solution.py:358
  154.7 2.2 copy-start.7
  168.6 35.3 %copy-start.9 = (s32[8]{0:T(128)S(1)}, s32[8]{0:T(128)}, u32[]{:S(2)}) copy-start(s32[8]{0:T(128)} %param.13) | copy-start | bytes 100
  168.6 35.3 %copy-start.10 = (s32[8]{0:T(128)S(1)}, s32[8]{0:T(128)}, u32[]{:S(2)}) copy-start(s32[8]{0:T(128)} %param.14) | copy-start | bytes 100
  220.3 9.9 %copy-start.1 = (bf16[256,2048]{1,0:T(8,128)(2,1)S(1)}, bf16[256,2048]{1,0:T(8,128)(2,1)}, u32[]{:S(2)}) copy-start(bf16[256,2048]{1,0:T(8,128)(2,1)} %param.12) | copy-start | bytes 3145732
Sparse Core Ops, SparseCore 0:
  17.3 43.7 all-gather.4
  114.3 40.3 all-gather.6
  204.1 22.1 all-gather.8

commit v2 on v0

v2 whole, which is shorter than its diff:
```python
import functools

import jax
import jax.numpy as jnp
from jax import lax
from jax.experimental import pallas as pl
from jax.experimental.pallas import tpu as pltpu
from jax.sharding import PartitionSpec as P

ROPE_BASE = 10000.0
NORM_EPS = 1e-5
BF16 = jnp.bfloat16
F32 = jnp.float32
TILE = 512
W_SLOTS = 10
D_SLOTS = 6
CORES = 2
ANY = pl.BlockSpec(memory_space=pl.ANY)
VMEM = pl.BlockSpec(memory_space=pltpu.VMEM)
SMEM = pl.BlockSpec(memory_space=pltpu.SMEM)
MESH = pl.DeviceIdType.MESH
NT = (((1,), (1,)), ((), ()))


def rms(wide):
    return (wide * lax.rsqrt(jnp.mean(wide * wide, axis=-1, keepdims=True) + NORM_EPS)).astype(BF16)


def rope_tile(vals, cos, sin, head_dim):
    wide = vals.astype(F32)
    width = wide.shape[1]
    half = head_dim // 2
    lane = lax.broadcasted_iota(jnp.int32, wide.shape, 1)
    other = jnp.where(lax.rem(lane, head_dim) < half, pltpu.roll(wide, width - half, 1), pltpu.roll(wide, half, 1))
    reps = width // cos.shape[1]
    return (wide * jnp.concatenate([cos] * reps, axis=1) + other * jnp.concatenate([sin] * reps, axis=1)).astype(BF16)


def mega_kernel(cfg, x_ref, y_ref, cos_ref, sin_ref, seg_ref, cosd_ref, sind_ref, len_ref, kc_ref, vc_ref,
                wq_ref, wo_ref, wg_ref, wu_ref, wd_ref,
                hid_ref, dec_ref, inst_ref, knv_ref,
                wbuf, dbuf, hin, h_ref, norm_ref, acc, xch, qkv, kvwin, dsend, rdec, cback, ctx, isend, kbuf, vbuf, hfin, mask_ref,
                wsem, dsem, insem, csem, xsend, xrecv, kvs, kvr, dss, dsr, cbs, cbr, iss, isr, ilo, fhs, fhr, fds, fdr, flo):
    side, tp, layers, head_dim, rep, slots = cfg
    s_me = lax.axis_index('side')
    t_me = lax.axis_index('tp')
    core = lax.rem(s_me, CORES)
    col = s_me // CORES
    chip = col * tp + t_me
    chips = side // CORES * tp
    partner = s_me + 1 - 2 * core
    model = h_ref.shape[1]
    rows = h_ref.shape[0]
    p_rows = mask_ref.shape[0]
    d_rows = (rows - p_rows) // CORES
    half_p = p_rows // 2
    window = kvwin.shape[1]
    q_loc = ctx.shape[2]
    group_w = rep * head_dim
    heads = q_loc // group_w
    kv_loc = heads * head_dim
    q_all = wo_ref.shape[1]
    kv_all = (wq_ref.shape[2] - q_all) // 2
    ff_loc = wg_ref.shape[2] // CORES
    n_ff = ff_loc // TILE
    n_q = q_loc // TILE
    n_o = q_loc // TILE
    n_w = 1 + n_q + 2 * n_ff
    n_d = n_o + n_ff

    def rc(src, dst, ssem, rsem, s_dev, t_dev):
        return pltpu.make_async_remote_copy(src_ref=src, dst_ref=dst, send_sem=ssem, recv_sem=rsem,
                                            device_id={'side': s_dev, 'tp': t_dev}, device_id_type=MESH)

    def at(base, size, unit):
        return pl.ds(pl.multiple_of(base, unit), size)

    def w_copies(idx):
        layer, pos = divmod(idx, n_w)
        slot = idx % W_SLOTS
        dst = wbuf.at[slot]
        if pos == 0:
            return [pltpu.make_async_copy(wq_ref.at[layer, :, at(q_all + core * kv_loc, kv_loc, 128)], dst.at[:, pl.ds(0, kv_loc)], wsem.at[slot, 0]),
                    pltpu.make_async_copy(wq_ref.at[layer, :, at(q_all + kv_all + core * kv_loc, kv_loc, 128)], dst.at[:, pl.ds(kv_loc, kv_loc)], wsem.at[slot, 1])]
        if pos <= n_q:
            return [pltpu.make_async_copy(wq_ref.at[layer, :, at(core * q_loc + (pos - 1) * TILE, TILE, TILE)], dst, wsem.at[slot, 0])]
        pos -= 1 + n_q
        src = (wg_ref, wu_ref)[pos % 2]
        return [pltpu.make_async_copy(src.at[layer, :, at(core * ff_loc + (pos // 2) * TILE, TILE, TILE)], dst, wsem.at[slot, 0])]

    def d_copies(idx):
        layer, pos = divmod(idx, n_d)
        slot = idx % D_SLOTS
        if pos < n_o:
            src = wo_ref.at[layer, at(core * q_loc + pos * TILE, TILE, TILE), :]
        else:
            src = wd_ref.at[layer, at(core * ff_loc + (pos - n_o) * TILE, TILE, TILE), :]
        return [pltpu.make_async_copy(src, dbuf.at[slot], dsem.at[slot])]

    def start_all(copies):
        for one in copies:
            one.start()

    def wait_all(copies):
        for one in copies:
            one.wait()

    def w_next(idx):
        if idx + W_SLOTS < layers * n_w:
            start_all(w_copies(idx + W_SLOTS))

    def d_next(idx):
        if idx + D_SLOTS < layers * n_d:
            start_all(d_copies(idx + D_SLOTS))

    def cache_copies(layer):
        return [pltpu.make_async_copy(kc_ref.at[layer], kbuf, csem.at[0]), pltpu.make_async_copy(vc_ref.at[layer], vbuf, csem.at[1])]

    x_mine = core == t_me // (tp // CORES)
    x_src = x_ref.at[at(lax.rem(t_me, tp // CORES) * p_rows, p_rows, p_rows), :]
    x_dst = hin.at[pl.ds(0, p_rows), :]
    y_src = y_ref.at[at(t_me * d_rows, d_rows, d_rows), :]
    y_dst = hin.at[at(p_rows + core * d_rows, d_rows, d_rows), :]
    x_local = pltpu.make_async_copy(x_src, x_dst, insem.at[0])
    y_local = pltpu.make_async_copy(y_src, y_dst, insem.at[1])
    x_far = rc(x_src, x_dst, insem.at[2], insem.at[3], partner, t_me)
    y_far = rc(y_src, y_dst, insem.at[4], insem.at[5], partner, t_me)

    start_all(w_copies(0))

    @pl.when(x_mine)
    def _():
        x_local.start()

    y_local.start()
    for idx in range(1, W_SLOTS):
        start_all(w_copies(idx))
        if idx == 2:
            start_all(cache_copies(0))
            start_all(d_copies(0))
            start_all(d_copies(1))
    for idx in range(2, D_SLOTS):
        start_all(d_copies(idx))

    barrier = pltpu.get_barrier_semaphore()
    for ds in range(side):
        for dt in range(tp):
            if ds or dt:
                pl.semaphore_signal(barrier, inc=1, device_id={'side': lax.rem(s_me + ds, side), 'tp': lax.rem(t_me + dt, tp)}, device_id_type=MESH)

    for layer in range(layers):
        kvwin[layer, 0:half_p, :] = jnp.zeros((half_p, kvwin.shape[2]), BF16)
        for dist in range(1, window // p_rows):
            lo = window - p_rows * (dist + 1)
            lo = max(lo, half_p)

            @pl.when(chip < dist)
            def _():
                hi = window - p_rows * dist
                kvwin[layer, lo:hi, :] = jnp.zeros((hi - lo, kvwin.shape[2]), BF16)

    key_row = (chip + 1) * p_rows - window + lax.broadcasted_iota(jnp.int32, mask_ref.shape, 1)
    q_row = chip * p_rows + lax.broadcasted_iota(jnp.int32, mask_ref.shape, 0)
    mask_ref[...] = jnp.where((key_row <= q_row) & (key_row >= seg_ref[...]), 1.0, 0.0)

    pl.semaphore_wait(barrier, side * tp - 1)

    @pl.when(x_mine)
    def _():
        x_far.start()

    y_far.start()

    @pl.when(x_mine)
    def _():
        x_local.wait()

    @pl.when(jnp.logical_not(x_mine))
    def _():
        x_far.wait_recv()

    y_local.wait()
    y_far.wait_recv()
    h_ref[...] = hin[...].astype(F32)

    diag = (lax.broadcasted_iota(jnp.int32, (d_rows, d_rows * head_dim), 1) // head_dim) == lax.broadcasted_iota(jnp.int32, (d_rows, d_rows * head_dim), 0)
    scale = head_dim ** -0.5

    def exchange(idx):
        return rc(acc, xch.at[idx], xsend.at[idx], xrecv.at[idx], partner, t_me)

    for layer in range(layers):
        w_base = layer * n_w
        d_base = layer * n_d
        norm_ref[...] = rms(h_ref[...])
        cos = cos_ref[...]
        sin = sin_ref[...]

        wait_all(w_copies(w_base))
        out = jnp.dot(norm_ref[...], wbuf[w_base % W_SLOTS], preferred_element_type=F32).astype(BF16)
        w_next(w_base)
        qkv[:, q_loc:] = out
        kvwin[layer, window - p_rows:, 0:kv_loc] = rope_tile(out[:p_rows, :kv_loc], cos, sin, head_dim)
        kvwin[layer, window - p_rows:, kv_loc:] = out[:p_rows, kv_loc:]

        def halo(dist):
            target = chip + dist
            last = window - p_rows * dist
            size = p_rows if last - p_rows >= half_p else half_p
            src = kvwin.at[layer, pl.ds(window - size, size), :]
            dst = kvwin.at[layer, pl.ds(last - size, size), :]
            return rc(src, dst, kvs.at[layer, dist - 1], kvr.at[layer, dist - 1], CORES * (target // tp) + core, lax.rem(target, tp))

        for dist in range(1, window // p_rows):
            @pl.when(chip + dist < chips)
            def _():
                halo(dist).start()

        for tile in range(n_q):
            idx = w_base + 1 + tile
            wait_all(w_copies(idx))
            out = jnp.dot(norm_ref[...], wbuf[idx % W_SLOTS], preferred_element_type=F32).astype(BF16)
            w_next(idx)
            sl = slice(tile * TILE, (tile + 1) * TILE)
            qkv[:p_rows, sl] = rope_tile(out[:p_rows], cos, sin, head_dim)
            qkv[p_rows:, sl] = out[p_rows:]

        for sub in range(CORES):
            for head in range(heads):
                r0 = p_rows + sub * d_rows
                kk = qkv[r0:r0 + d_rows, q_loc + head * head_dim:q_loc + (head + 1) * head_dim]
                vv = qkv[r0:r0 + d_rows, q_loc + kv_loc + head * head_dim:q_loc + kv_loc + (head + 1) * head_dim]
                dsend[layer, sub, head, :, 0:group_w] = qkv[r0:r0 + d_rows, head * group_w:(head + 1) * group_w]
                dsend[layer, sub, head, :, group_w:] = jnp.concatenate([kk, vv], axis=1)

        def forward(dt, dc):
            s2 = lax.rem(core + dc, CORES)
            t2 = lax.rem(t_me + dt, tp)
            return rc(dsend.at[layer, s2, t2], rdec.at[layer, t_me, core], dss.at[layer, dt * CORES + dc], dsr.at[layer, dt * CORES + dc], col * CORES + s2, t2)

        for dt in range(tp):
            for dc in range(CORES):
                if dt or dc:
                    forward(dt, dc).start()
        rdec[layer, t_me, core] = dsend[layer, core, t_me]

        def backward(dt, dc):
            t2 = lax.rem(t_me + tp - dt, tp)
            c2 = lax.rem(core + dc, CORES)
            dst = ctx.at[layer, at(p_rows + core * d_rows, d_rows, d_rows), at(t_me * group_w, group_w, group_w)]
            return rc(cback.at[layer, dt * CORES + dc], dst, cbs.at[layer, dt * CORES + dc], cbr.at[layer, dt * CORES + dc], col * CORES + c2, t2)

        wait_all(cache_copies(layer))
        for dt in range(tp):
            for dc in range(CORES):
                t2 = lax.rem(t_me + tp - dt, tp)
                c2 = lax.rem(core + dc, CORES)
                if dt or dc:
                    forward(dt, dc).wait_recv()
                raw = rdec[layer, t2, c2]
                roped = rope_tile(raw, cosd_ref[t2], sind_ref[t2], head_dim)
                k_new = roped[:, group_w:group_w + head_dim]
                v_new = raw[:, group_w + head_dim:]
                knv_ref[layer, t2, c2] = jnp.concatenate([k_new, v_new], axis=1)
                q_wide = roped[:, :group_w].astype(F32) * scale
                q_parts = [q_wide[:, r * head_dim:(r + 1) * head_dim] for r in range(rep)]
                lhs = jnp.concatenate([jnp.where(diag, jnp.concatenate([jnp.concatenate([part, part], axis=1)] * (d_rows // 2), axis=1), 0.0) for part in q_parts], axis=0).astype(BF16)
                k_part = kbuf[at(t2 * d_rows, d_rows, d_rows), c2].reshape(d_rows * head_dim, kbuf.shape[3])
                v_part = vbuf[at(t2 * d_rows, d_rows, d_rows), c2].reshape(d_rows * head_dim, vbuf.shape[3])
                scores = jnp.dot(lhs, k_part, preferred_element_type=F32)
                s_new = jnp.sum(jnp.concatenate(q_parts, axis=0) * jnp.concatenate([k_new.astype(F32)] * rep, axis=0), axis=-1, keepdims=True)
                where_new = len_ref[t2]
                pos = lax.broadcasted_iota(jnp.int32, scores.shape, 1)
                scores = jnp.where(pos < where_new, scores, -1e30)
                scores = jnp.where(pos == where_new, s_new, scores)
                scores = jnp.exp(scores - jnp.max(scores, axis=-1, keepdims=True))
                prob = (scores * (1.0 / jnp.sum(scores, axis=-1, keepdims=True))).astype(BF16).astype(F32)
                p_new = jnp.sum(jnp.where(pos == where_new, prob, 0.0), axis=-1, keepdims=True)
                p_old = jnp.where(pos == where_new, 0.0, prob).astype(BF16)
                full = lax.dot_general(p_old, v_part, NT, preferred_element_type=F32)
                full = jnp.where(jnp.concatenate([diag] * rep, axis=0), full, 0.0)
                fold = full[:, 0:128]
                for piece in range(1, full.shape[1] // 128):
                    fold = fold + full[:, piece * 128:(piece + 1) * 128]
                got = fold[:, :head_dim] + fold[:, head_dim:] + p_new * jnp.concatenate([v_new.astype(F32)] * rep, axis=0)
                got = jnp.concatenate([got[r * d_rows:(r + 1) * d_rows] for r in range(rep)], axis=1).astype(BF16)
                if dt or dc:
                    cback[layer, dt * CORES + dc] = got
                    backward(dt, dc).start()
                else:
                    ctx[layer, at(p_rows + core * d_rows, d_rows, d_rows), at(t_me * group_w, group_w, group_w)] = got
        if layer + 1 < layers:
            start_all(cache_copies(layer + 1))

        for dist in range(1, window // p_rows):
            @pl.when(chip >= dist)
            def _():
                halo(dist).wait_recv()

        allowed = mask_ref[...] > 0.5
        for head in range(heads):
            k_head = kvwin[layer, :, head * head_dim:(head + 1) * head_dim]
            v_head = kvwin[layer, :, kv_loc + head * head_dim:kv_loc + (head + 1) * head_dim]
            outs = []
            for sub in range(rep):
                q0 = head * group_w + sub * head_dim
                q_part = (qkv[:p_rows, q0:q0 + head_dim].astype(F32) * scale).astype(BF16)
                scores = lax.dot_general(q_part, k_head, NT, preferred_element_type=F32)
                scores = jnp.where(allowed, scores, -1e30)
                scores = jnp.exp(scores - jnp.max(scores, axis=-1, keepdims=True))
                prob = (scores * (1.0 / jnp.sum(scores, axis=-1, keepdims=True))).astype(BF16)
                outs.append(jnp.dot(prob, v_head, preferred_element_type=F32).astype(BF16))
            ctx[layer, 0:p_rows, head * group_w:(head + 1) * group_w] = jnp.concatenate(outs, axis=1)
            isend[layer, head] = jnp.concatenate([k_head[window - p_rows:], v_head[window - p_rows:]], axis=1)

        def install(ds, dt):
            s2 = lax.rem(s_me + ds, side)
            t2 = lax.rem(t_me + dt, tp)
            return rc(isend.at[layer, t2], inst_ref.at[layer, core, at(chip * p_rows, p_rows, p_rows), :], iss.at[layer, ds * tp + dt], isr.at[layer, ds * tp + dt], s2, t2)

        def install_own():
            return pltpu.make_async_copy(isend.at[layer, t_me], inst_ref.at[layer, core, at(chip * p_rows, p_rows, p_rows), :], ilo.at[layer])

        for ds in range(side):
            for dt in range(tp):
                if ds or dt:
                    install(ds, dt).start()
        install_own().start()

        for dt in range(tp):
            for dc in range(CORES):
                if dt or dc:
                    backward(dt, dc).wait_recv()

        if layer:
            exchange(2 * layer - 1).wait_send()
        for tile in range(n_o):
            idx = d_base + tile
            wait_all(d_copies(idx))
            part = jnp.dot(ctx[layer, :, tile * TILE:(tile + 1) * TILE], dbuf[idx % D_SLOTS], preferred_element_type=F32)
            if tile == 0:
                acc[...] = part
            else:
                acc[...] += part
            d_next(idx)
        exchange(2 * layer).start()
        exchange(2 * layer).wait()
        h_ref[...] = (h_ref[...] + (acc[...] + xch[2 * layer]).astype(BF16).astype(F32)).astype(BF16).astype(F32)
        norm_ref[...] = rms(h_ref[...])

        for chunk in range(n_ff):
            idx = w_base + 1 + n_q + 2 * chunk
            wait_all(w_copies(idx))
            gate = jnp.dot(norm_ref[...], wbuf[idx % W_SLOTS], preferred_element_type=F32).astype(BF16).astype(F32)
            w_next(idx)
            wait_all(w_copies(idx + 1))
            upper = jnp.dot(norm_ref[...], wbuf[(idx + 1) % W_SLOTS], preferred_element_type=F32).astype(BF16).astype(F32)
            w_next(idx + 1)
            act = (jax.nn.silu(gate) * upper).astype(BF16)
            d_idx = d_base + n_o + chunk
            wait_all(d_copies(d_idx))
            part = jnp.dot(act, dbuf[d_idx % D_SLOTS], preferred_element_type=F32)
            if chunk == 0:
                acc[...] = part
            else:
                acc[...] += part
            d_next(d_idx)
        exchange(2 * layer + 1).start()
        exchange(2 * layer + 1).wait_recv()
        h_ref[...] = (h_ref[...] + (acc[...] + xch[2 * layer + 1]).astype(BF16).astype(F32)).astype(BF16).astype(F32)

        for dist in range(1, window // p_rows):
            @pl.when(chip + dist < chips)
            def _():
                halo(dist).wait_send()
        for dt in range(tp):
            for dc in range(CORES):
                if dt or dc:
                    forward(dt, dc).wait_send()
                    backward(dt, dc).wait_send()
        for ds in range(side):
            for dt in range(tp):
                if ds or dt:
                    install(ds, dt).wait()
        install_own().wait()

    exchange(2 * layers - 1).wait_send()

    @pl.when(x_mine)
    def _():
        x_far.wait_send()

    y_far.wait_send()

    hfin[...] = h_ref[...].astype(BF16)
    half_t = tp // CORES
    own_hid = core == t_me // half_t
    hid_src = hfin.at[at(core * half_p, half_p, half_p), :]
    hid_dst = hid_ref.at[at(lax.rem(t_me, half_t) * p_rows + core * half_p, half_p, half_p), :]
    dec_src = hfin.at[at(p_rows + core * d_rows, d_rows, d_rows), :]
    dec_dst = dec_ref.at[at(t_me * d_rows, d_rows, d_rows), :]
    hid_local = pltpu.make_async_copy(hid_src, hid_dst, flo.at[0])
    dec_local = pltpu.make_async_copy(dec_src, dec_dst, flo.at[1])
    piece_me = lax.rem(t_me, half_t) * CORES + core

    def hid_far(dt):
        return rc(hid_src, hid_dst, fhs.at[dt], fhr.at[piece_me], col * CORES + t_me // half_t, lax.rem(t_me + dt, tp))

    def dec_far(dt):
        return rc(dec_src, dec_dst, fds.at[dt], fdr.at[dt], s_me, lax.rem(t_me + dt, tp))

    for dt in range(1, tp):
        hid_far(dt).start()
        dec_far(dt).start()

    @pl.when(own_hid)
    def _():
        hid_local.start()

    @pl.when(jnp.logical_not(own_hid))
    def _():
        hid_far(0).start()

    dec_local.start()
    for dt in range(1, tp):
        hid_far(dt).wait_send()
        dec_far(dt).wait()

    @pl.when(own_hid)
    def _():
        hid_local.wait()

    @pl.when(jnp.logical_not(own_hid))
    def _():
        hid_far(0).wait_send()

    dec_local.wait()
    for sub in range(half_t):
        for c2 in range(CORES):
            mine = (core * half_t + sub == t_me) & (core == c2)

            @pl.when(jnp.logical_not(mine))
            def _():
                rc(hid_src, hid_ref.at[pl.ds(sub * p_rows + c2 * half_p, half_p), :], fhs.at[0], fhr.at[sub * CORES + c2], s_me, t_me).wait_recv()


def finish_kernel(head_dim, slots, blk_ref, len_ref, inst_ref, kn_ref, vn_ref, k_ref, v_ref, kp_ref, vp_ref, kout_ref, vout_ref, ibuf, isem):
    layer = pl.program_id(0)
    step = pl.program_id(1)
    t_len = k_ref.shape[1]
    pairs = k_ref.shape[0] // head_dim
    batch = pairs // slots
    win = ibuf.shape[1]
    max_req = kp_ref.shape[1]

    def grab(lay):
        return pltpu.make_async_copy(inst_ref.at[lay, :, pl.ds(pl.multiple_of(blk_ref[0], 16), win), :], ibuf, isem)

    @pl.when(step == 0)
    def _():
        grab(layer).start()

    t_iota = lax.broadcasted_iota(jnp.int32, (head_dim, t_len), 1)
    for pair in range(pairs):
        here = t_iota == len_ref[step * batch + pair // slots]
        sl = slice(pair * head_dim, (pair + 1) * head_dim)
        kout_ref[sl, :] = jnp.where(here, kn_ref[:, pair:pair + 1].astype(F32), k_ref[sl, :].astype(F32)).astype(BF16)
        vout_ref[sl, :] = jnp.where(here, vn_ref[:, pair:pair + 1].astype(F32), v_ref[sl, :].astype(F32)).astype(BF16)

    @pl.when(step == 0)
    def _():
        grab(layer).wait()
        row = blk_ref[0] + lax.broadcasted_iota(jnp.int32, (win, max_req), 0)
        want = lax.broadcasted_iota(jnp.int32, (win, max_req), 1)
        pick = jnp.where((row - blk_ref[1] == want) & (want < blk_ref[2]), 1.0, 0.0).astype(BF16)
        for slot in range(slots):
            both = lax.dot_general(ibuf[slot], pick, (((0,), (0,)), ((), ())), preferred_element_type=F32).astype(BF16)
            kp_ref[slot * head_dim:(slot + 1) * head_dim, :] = both[:head_dim]
            vp_ref[slot * head_dim:(slot + 1) * head_dim, :] = both[head_dim:]


def solution(mesh):
    tp = mesh.shape['tp']
    side = mesh.shape['side']
    rows_spec = P(('pair', 'side'), None)
    batch_spec = P(('pair', 'side'), None, None)
    cache_spec = P(('pair', 'side'), None, None, None, 'tp', None)
    prompt_spec = P(('pair', 'side'), None, None, 'tp', None)

    def local_step(x_loc, req_len, dest, w_qkv, w_out, w_gate, w_up, w_down, y_loc, kc_loc, vc_loc, clen_loc):
        s_idx = lax.axis_index('side')
        t_idx = lax.axis_index('tp')
        layers = w_qkv.shape[0]
        head_dim = kc_loc.shape[-1]
        slots = kc_loc.shape[-2]
        t_len = kc_loc.shape[3]
        batch = y_loc.shape[1]
        kv_heads = slots * tp
        rep = w_out.shape[1] // head_dim // kv_heads
        model = x_loc.shape[1]
        prompt_rows = x_loc.shape[0]
        seq_len = prompt_rows * side
        max_req = 2 * prompt_rows - prompt_rows // 4
        p_rows = prompt_rows * CORES // tp
        d_rows = batch // tp
        rows = p_rows + CORES * d_rows
        q_loc = w_out.shape[1] // CORES
        kv_loc = kv_heads // CORES * head_dim
        heads = kv_heads // CORES
        window = -(-(max_req - 1) // p_rows) * p_rows + p_rows
        group_w = rep * head_dim

        chip = s_idx // CORES * tp + t_idx
        ids = jnp.arange(side)
        ends = jnp.sum(jnp.where(ids[None, :] <= ids[:, None], req_len[None, :], 0), axis=1)
        row_ids = chip * p_rows + jnp.arange(p_rows)
        seg_start = jnp.sum(jnp.where(row_ids[:, None] >= ends[None, :], req_len[None, :], 0), axis=1)
        lengths = clen_loc[0]
        half = head_dim // 2
        inv_freq = ROPE_BASE ** (-jnp.arange(half, dtype=F32) / half)
        positions = jnp.concatenate([row_ids - seg_start, lengths])
        angles = positions.astype(F32)[:, None] * inv_freq
        cos = jnp.cos(angles)
        sin = jnp.sin(angles)
        cos = jnp.concatenate([cos] * 4, axis=1)
        sin = jnp.concatenate([-sin, sin] * 2, axis=1)
        cos_d = cos[p_rows:].reshape(tp, d_rows, 2 * head_dim)
        sin_d = sin[p_rows:].reshape(tp, d_rows, 2 * head_dim)
        len_rows = jnp.broadcast_to(lengths.reshape(tp, 1, d_rows), (tp, rep, d_rows)).reshape(tp, rep * d_rows, 1)
        kc = jnp.transpose(kc_loc[0], (0, 1, 3, 4, 2))
        vc = jnp.transpose(vc_loc[0], (0, 1, 3, 4, 2))

        dma = pltpu.SemaphoreType.DMA
        n_peer = tp * CORES
        hid, dec, inst, knv = pl.pallas_call(
            functools.partial(mega_kernel, (side, tp, layers, head_dim, rep, slots)),
            out_shape=[jax.ShapeDtypeStruct((prompt_rows, model), BF16), jax.ShapeDtypeStruct((batch, model), BF16),
                       jax.ShapeDtypeStruct((layers, CORES, seq_len, 2 * head_dim), BF16),
                       jax.ShapeDtypeStruct((layers, tp, CORES, d_rows, 2 * head_dim), BF16)],
            in_specs=[ANY, ANY, VMEM, VMEM, VMEM, VMEM, VMEM, VMEM, ANY, ANY, ANY, ANY, ANY, ANY, ANY],
            out_specs=[ANY, ANY, ANY, VMEM],
            scratch_shapes=[
                pltpu.VMEM((W_SLOTS, model, TILE), BF16),
                pltpu.VMEM((D_SLOTS, TILE, model), BF16),
                pltpu.VMEM((rows, model), BF16),
                pltpu.VMEM((rows, model), F32),
                pltpu.VMEM((rows, model), BF16),
                pltpu.VMEM((rows, model), F32),
                pltpu.VMEM((2 * layers, rows, model), F32),
                pltpu.VMEM((rows, q_loc + 2 * kv_loc), BF16),
                pltpu.VMEM((layers, window, 2 * kv_loc), BF16),
                pltpu.VMEM((layers, CORES, heads, d_rows, group_w + 2 * head_dim), BF16),
                pltpu.VMEM((layers, tp, CORES, d_rows, group_w + 2 * head_dim), BF16),
                pltpu.VMEM((layers, n_peer, d_rows, group_w), BF16),
                pltpu.VMEM((layers, rows, q_loc), BF16),
                pltpu.VMEM((layers, heads, p_rows, 2 * head_dim), BF16),
                pltpu.VMEM((batch, slots, head_dim, t_len), BF16),
                pltpu.VMEM((batch, slots, head_dim, t_len), BF16),
                pltpu.VMEM((rows, model), BF16),
                pltpu.VMEM((p_rows, window), F32),
                dma((W_SLOTS, 2)), dma((D_SLOTS,)), dma((6,)), dma((2,)),
                dma((2 * layers,)), dma((2 * layers,)),
                dma((layers, 4)), dma((layers, 4)),
                dma((layers, n_peer)), dma((layers, n_peer)),
                dma((layers, n_peer)), dma((layers, n_peer)),
                dma((layers, side * tp)), dma((layers, side * tp)), dma((layers,)),
                dma((tp,)), dma((tp,)), dma((tp,)), dma((tp,)), dma((2,)),
            ],
            compiler_params=pltpu.CompilerParams(collective_id=0, has_side_effects=True, vmem_limit_bytes=67043328),
            name="mega",
        )(x_loc, y_loc[0], cos[:p_rows], sin[:p_rows], seg_start[:, None].astype(jnp.int32), cos_d, sin_d, len_rows, kc, vc,
          w_qkv, w_out, w_gate, w_up, w_down)

        mine = dest == s_idx
        start = jnp.sum(jnp.where(mine, ends - req_len, 0))
        length = jnp.sum(jnp.where(mine, req_len, 0))
        win = 512
        blk = jnp.minimum(start // 64 * 64, seq_len - win)
        steps = 8
        depth = batch * slots * head_dim
        per = batch * slots // steps
        new = jnp.transpose(knv, (0, 1, 3, 2, 4)).reshape(layers, steps, per, 2 * head_dim)
        new = jnp.transpose(new, (0, 1, 3, 2))
        kc2 = kc.reshape(layers, depth, t_len)
        vc2 = vc.reshape(layers, depth, t_len)
        cache_b = pl.BlockSpec((None, depth // steps, t_len), lambda l, i: (l, i, 0))
        prompt_b = pl.BlockSpec((None, slots * head_dim, max_req), lambda l, i: (l, 0, 0))

        def col_b(which):
            return pl.BlockSpec((None, None, head_dim, per), lambda l, i: (l, i, which, 0))

        kp, vp, k_out, v_out = pl.pallas_call(
            functools.partial(finish_kernel, head_dim, slots),
            out_shape=[jax.ShapeDtypeStruct((layers, slots * head_dim, max_req), BF16)] * 2 + [jax.ShapeDtypeStruct(kc2.shape, BF16)] * 2,
            grid=(layers, steps),
            in_specs=[SMEM, SMEM, ANY, col_b(0), col_b(1), cache_b, cache_b],
            out_specs=[prompt_b, prompt_b, cache_b, cache_b],
            scratch_shapes=[pltpu.VMEM((slots, win, 2 * head_dim), BF16), dma],
            compiler_params=pltpu.CompilerParams(vmem_limit_bytes=40 * 2**20),
            name="finish",
        )(jnp.stack([blk, start, length]).astype(jnp.int32), lengths, inst, new, new, kc2, vc2)

        def cache_back(arr):
            return jnp.transpose(arr.reshape(layers, batch, slots, head_dim, t_len), (0, 1, 4, 2, 3))[None]

        def prompt_back(arr):
            return jnp.transpose(arr.reshape(layers, slots, head_dim, max_req), (0, 3, 1, 2))[None]

        return hid, dec[None], prompt_back(kp), prompt_back(vp), cache_back(k_out), cache_back(v_out)

    return jax.shard_map(local_step, mesh=mesh,
                         in_specs=(rows_spec, P('pair'), P('pair'), P(), P(), P(), P(), P(), batch_spec, cache_spec, cache_spec, rows_spec),
                         out_specs=(rows_spec, batch_spec, prompt_spec, prompt_spec, cache_spec, cache_spec),
                         check_vma=False)
```

time: 3670 us -> 156 us (0.04)
  the two profiles are of different devices: /device:TPU:98 before, /device:TPU:102 now
where the time goes in v2:
time: 156 us; the launch traced here: 153 us
  Pallas kernels  125 us (80%)
  local copies, waits for them, and re-layouts  15.7 us (10%)
  other arithmetic  8.09 us (5%)
  between operations  3.46 us (2%)
    pallas_call x1, Pallas kernels, local_step(): pl.pallas_call(functools.partial(mega_kernel, (side, tp, layers, head_dim...  115 us
    unnamed x13, local copies, waits for them, and re-layouts  11.7 us
    pallas_call x1, Pallas kernels, local_step(): pl.pallas_call(functools.partial(finish_kernel, head_dim, slots), out_sha...  10 us

profile of v2, /device:TPU:102, one launch (start us, length us, event | category | flops | bytes accessed | tf_op | source)
XLA Modules:
  0.0 152.6 jit_solution(17052387624745704083)
XLA Ops:
  0.6 0.5 broadcast.22
  1.2 1.3 reduce.3
  2.5 0.8 select_reduce_fusion.1
  3.3 0.7 select_reduce_fusion
  4.0 1.3 fusion.1
  7.9 1.9 %pad_add_fusion.blk_ref = s32[3]{0:T(128)} fusion(s32[1]{0:T(128)} %bitcast.12, s32[1]{0:T(128)} %bitcast.11, s32[1]{0:T(128)} %bitcast.10), kind=kLoop, calls=%fused_computation.15 | loop fusion | flops 6 | bytes 24 | tf_op jit(solution)/shard_map/stack | solution.py:601
  9.8 0.7 add_convert_fusion
  10.5 0.1 broadcast_in_dim.67
  10.6 0.7 copy.23.seg_ref
  11.3 0.8 reshape.81.len_ref
  12.1 0.4 fusion
  12.5 0.8 pad_maximum_fusion.2
  13.3 0.2 pad_maximum_fusion
  13.5 0.6 slice.16.cos_ref
  14.1 0.6 slice.17.sin_ref
  14.7 115.3 %mega.1 = (bf16[256,2048]{1,0:T(8,128)(2,1)}, bf16[64,2048]{1,0:T(8,128)(2,1)}, bf16[2,2,2048,128]{3,2,1,0:T(8,128)(2,1)}, bf16[2,4,2,16,128]{4,3,2,1,0:T(8,128)(2,1)}) custom-call(bf16[256,2048]{1,0:T(8,128)(2,1)} %x_ref.1, bf16[64,2048]{1,0:T(8,128)(2,1)} %bitcast.50, f32[128,128]{1,0:T(8,128)} %slice.16.cos_ref, f32[128,128]{1,0:T(8,128)} %slice.17.sin_ref, ...), custom_call_target="tpu_custom_call" | custom-call | tf_op jit(solution)/shard_map/mega/pallas_call | solution.py:535
  130.0 0.9 copy.25
  130.9 0.3 copy.26
  131.2 0.0 copy-start
  131.2 2.2 %copy-done = bf16[1,2,64,128,2,64]{3,5,4,2,1,0:T(8,128)(2,1)S(1)} copy-done((bf16[1,2,64,128,2,64]{3,5,4,2,1,0:T(8,128)(2,1)S(1)}, bf16[1,2,64,128,2,64]{3,5,4,2,1,0:T(8,128)(2,1)}, u32[]{:S(2)}) %copy-start) | copy-done | bytes 4194328
  133.4 0.0 copy-start.1
  133.4 2.2 %copy-done.1 = bf16[1,2,64,128,2,64]{3,5,4,2,1,0:T(8,128)(2,1)S(1)} copy-done((bf16[1,2,64,128,2,64]{3,5,4,2,1,0:T(8,128)(2,1)S(1)}, bf16[1,2,64,128,2,64]{3,5,4,2,1,0:T(8,128)(2,1)}, u32[]{:S(2)}) %copy-start.1) | copy-done | bytes 4194328
  135.6 0.0 copy-start.2
  135.6 1.6 %copy-done.2 = bf16[2,2,2048,128]{3,2,1,0:T(8,128)(2,1)S(1)} copy-done((bf16[2,2,2048,128]{3,2,1,0:T(8,128)(2,1)S(1)}, bf16[2,2,2048,128]{3,2,1,0:T(8,128)(2,1)}, u32[]{:S(2)}) %copy-start.2) | copy-done | bytes 2097176
  137.2 0.0 copy-start.3
  137.2 0.7 copy-done.3
  137.8 0.0 copy-start.4
  137.8 0.6 copy-done.4
  138.4 10.0 %finish.1 = (bf16[2,128,448]{2,1,0:T(8,128)(2,1)}, bf16[2,128,448]{2,1,0:T(8,128)(2,1)}, bf16[2,8192,128]{2,1,0:T(8,128)(2,1)}, bf16[2,8192,128]{2,1,0:T(8,128)(2,1)}) custom-call(s32[3]{0:T(128)S(1)} %copy-done.4, s32[64]{0:T(128)S(1)} %bitcast.49, bf16[2,2,2048,128]{3,2,1,0:T(8,128)(2,1)S(1)} %copy-done.2, bf16[2,8,128,16]{3,2,1,0:T(8,128)(2,1)S(1)} %bitcast.46, ...), custom_call_target="tpu_custom_call" | custom-call | tf_op jit(solution)/shard_map/finish/pallas_call | solution.py:592
  148.5 2.3 %copy.29 = bf16[256,2048]{1,0:T(8,128)(2,1)} copy(bf16[256,2048]{1,0:T(8,128)(2,1)} %get-tuple-element.37) | data formatting | bytes 2097152
  150.8 1.7 %copy.30 = bf16[1,64,2048]{2,1,0:T(8,128)(2,1)} copy(bf16[1,64,2048]{2,1,0:T(8,128)(2,1)} %bitcast.52) | data formatting | bytes 524288
  (4 shorter events, 0.0 us)
Async XLA Ops:
  131.2 2.2 %copy-start = (bf16[1,2,64,128,2,64]{3,5,4,2,1,0:T(8,128)(2,1)S(1)}, bf16[1,2,64,128,2,64]{3,5,4,2,1,0:T(8,128)(2,1)}, u32[]{:S(2)}) copy-start(bf16[1,2,64,128,2,64]{3,5,4,2,1,0:T(8,128)(2,1)} %param.21) | copy-start | bytes 12582916
  133.4 2.2 %copy-start.1 = (bf16[1,2,64,128,2,64]{3,5,4,2,1,0:T(8,128)(2,1)S(1)}, bf16[1,2,64,128,2,64]{3,5,4,2,1,0:T(8,128)(2,1)}, u32[]{:S(2)}) copy-start(bf16[1,2,64,128,2,64]{3,5,4,2,1,0:T(8,128)(2,1)} %param.22) | copy-start | bytes 12582916
  135.6 1.6 %copy-start.2 = (bf16[2,2,2048,128]{3,2,1,0:T(8,128)(2,1)S(1)}, bf16[2,2,2048,128]{3,2,1,0:T(8,128)(2,1)}, u32[]{:S(2)}) copy-start(bf16[2,2,2048,128]{3,2,1,0:T(8,128)(2,1)} %get-tuple-element.16.inst_ref) | copy-start | bytes 6291460
  137.2 0.7 copy-start.3
  137.8 0.6 copy-start.4

commit v3 on v2

v3 whole, which is shorter than its diff:
```python
import functools
import math

import jax
import jax.numpy as jnp
from jax import lax
from jax.experimental import pallas as pl
from jax.experimental.pallas import tpu as pltpu
from jax.sharding import PartitionSpec as P

ROPE_BASE = 10000.0
NORM_EPS = 1e-5
BF16 = jnp.bfloat16
F32 = jnp.float32
TILE = 512
W_SLOTS = 18
CORES = 2
ANY = pl.BlockSpec(memory_space=pl.ANY)
VMEM = pl.BlockSpec(memory_space=pltpu.VMEM)
SMEM = pl.BlockSpec(memory_space=pltpu.SMEM)
MESH = pl.DeviceIdType.MESH
NT = (((1,), (1,)), ((), ()))


def rms(wide):
    return (wide * lax.rsqrt(jnp.mean(wide * wide, axis=-1, keepdims=True) + NORM_EPS)).astype(BF16)


def rope_tile(vals, cos, sin, head_dim):
    wide = vals.astype(F32)
    width = wide.shape[1]
    half = head_dim // 2
    lane = lax.broadcasted_iota(jnp.int32, wide.shape, 1)
    other = jnp.where(lax.rem(lane, head_dim) < half, pltpu.roll(wide, width - half, 1), pltpu.roll(wide, half, 1))
    reps = width // cos.shape[1]
    return (wide * jnp.concatenate([cos] * reps, axis=1) + other * jnp.concatenate([sin] * reps, axis=1)).astype(BF16)


def to_column(row, count, owner):
    n = row.shape[1]
    j = lax.broadcasted_iota(jnp.int32, (count, n), 0)
    return jnp.sum(jnp.where(lax.broadcasted_iota(jnp.int32, (count, n), 1) == owner(j), row.astype(F32), 0.0), axis=-1, keepdims=True)


def mega_kernel(cfg, req_ref, clen_ref, x_ref, y_ref, kc_ref, vc_ref, wq_ref, wo_ref, wg_ref, wu_ref, wd_ref,
                hid_ref, dec_ref, inst_ref, knv_ref,
                wbuf, hin, h_ref, norm_ref, acc, xch, qkv, kvwin, dsend, rdec, cback, ctx, isend, kbuf, vbuf, act_ref, gu, mask_ref, cos_ref, sin_ref, cosd_ref, sind_ref, len_ref,
                wsem, insem, csem, xsend, xrecv, kvs, kvr, dss, dsr, cbs, cbr, i1s, i1r, i2s, i2r, i3s, i3r, ilo, fhs, fhr, fds, fdr, hws, dws, flo):
    side, tp, layers, head_dim, rep, slots = cfg
    s_me = lax.axis_index('side')
    t_me = lax.axis_index('tp')
    core = lax.rem(s_me, CORES)
    col = s_me // CORES
    chip = col * tp + t_me
    chips = side // CORES * tp
    partner = s_me + 1 - 2 * core
    model = h_ref.shape[1]
    rows = h_ref.shape[0]
    p_rows = mask_ref.shape[0]
    d_rows = (rows - p_rows) // CORES
    half_p = p_rows // 2
    window = kvwin.shape[1]
    q_loc = ctx.shape[2]
    group_w = rep * head_dim
    heads = q_loc // group_w
    kv_loc = heads * head_dim
    q_all = wo_ref.shape[1]
    kv_all = (wq_ref.shape[2] - q_all) // 2
    ff_loc = wg_ref.shape[2] // CORES
    n_ff = ff_loc // TILE
    n_q = q_loc // TILE
    n_o = model * q_loc // (TILE * model)
    n_deep = ff_loc // model
    n_dn = model // TILE
    base_o = 1 + n_q
    base_g = base_o + n_o
    base_d = base_g + 2 * n_ff
    n_w = base_d + n_dn * n_deep

    def rc(src, dst, ssem, rsem, s_dev, t_dev):
        return pltpu.make_async_remote_copy(src_ref=src, dst_ref=dst, send_sem=ssem, recv_sem=rsem,
                                            device_id={'side': s_dev, 'tp': t_dev}, device_id_type=MESH)

    def at(base, size, unit):
        return pl.ds(pl.multiple_of(base, unit), size)

    def w_copies(idx):
        layer, pos = divmod(idx, n_w)
        slot = idx % W_SLOTS
        dst = wbuf.at[slot]
        if pos == 0:
            return [pltpu.make_async_copy(wq_ref.at[layer, :, at(q_all + core * kv_loc, kv_loc, 128)], dst.at[:, pl.ds(0, kv_loc)], wsem.at[slot, 0]),
                    pltpu.make_async_copy(wq_ref.at[layer, :, at(q_all + kv_all + core * kv_loc, kv_loc, 128)], dst.at[:, pl.ds(kv_loc, kv_loc)], wsem.at[slot, 1])]
        if pos < base_o:
            return [pltpu.make_async_copy(wq_ref.at[layer, :, at(core * q_loc + (pos - 1) * TILE, TILE, TILE)], dst, wsem.at[slot, 0])]
        if pos < base_g:
            pos -= base_o
            return [pltpu.make_async_copy(wo_ref.at[layer, at(core * q_loc, q_loc, q_loc), pl.ds((2 * pos + part) * TILE, TILE)], dst.at[pl.ds(part * q_loc, q_loc), :], wsem.at[slot, part]) for part in range(2)]
        if pos < base_d:
            pos -= base_g
            src = (wg_ref, wu_ref)[pos % 2]
            return [pltpu.make_async_copy(src.at[layer, :, at(core * ff_loc + (pos // 2) * TILE, TILE, TILE)], dst, wsem.at[slot, 0])]
        pos -= base_d
        return [pltpu.make_async_copy(wd_ref.at[layer, at(core * ff_loc + pos % n_deep * model, model, model), pl.ds(pos // n_deep * TILE, TILE)], dst, wsem.at[slot, 0])]

    def start_all(copies):
        for one in copies:
            one.start()

    def wait_all(copies):
        for one in copies:
            one.wait()

    def w_next(idx):
        if idx + W_SLOTS < layers * n_w:
            start_all(w_copies(idx + W_SLOTS))

    def cache_copies(layer):
        return [pltpu.make_async_copy(kc_ref.at[layer], kbuf, csem.at[0]), pltpu.make_async_copy(vc_ref.at[layer], vbuf, csem.at[1])]

    x_mine = core == t_me // (tp // CORES)
    x_src = x_ref.at[at(lax.rem(t_me, tp // CORES) * p_rows, p_rows, p_rows), :]
    x_dst = hin.at[pl.ds(0, p_rows), :]
    y_src = y_ref.at[at(t_me * d_rows, d_rows, d_rows), :]
    y_dst = hin.at[at(p_rows + core * d_rows, d_rows, d_rows), :]
    x_local = pltpu.make_async_copy(x_src, x_dst, insem.at[0])
    y_local = pltpu.make_async_copy(y_src, y_dst, insem.at[1])
    x_far = rc(x_dst, x_dst, insem.at[2], insem.at[3], partner, t_me)
    y_far = rc(y_dst, y_dst, insem.at[4], insem.at[5], partner, t_me)

    @pl.when(x_mine)
    def _():
        x_local.start()

    y_local.start()
    start_all(w_copies(0))

    barrier = pltpu.get_barrier_semaphore()
    for ds in range(side):
        for dt in range(tp):
            if ds or dt:
                pl.semaphore_signal(barrier, inc=1, device_id={'side': lax.rem(s_me + ds, side), 'tp': lax.rem(t_me + dt, tp)}, device_id_type=MESH)

    for idx in range(1, W_SLOTS):
        start_all(w_copies(idx))
        if idx == 2:
            start_all(cache_copies(0))

    for layer in range(layers):
        kvwin[layer, 0:half_p, :] = jnp.zeros((half_p, kvwin.shape[2]), BF16)
        for dist in range(1, window // p_rows):
            lo = max(window - p_rows * (dist + 1), half_p)

            @pl.when(chip < dist)
            def _():
                hi = window - p_rows * dist
                kvwin[layer, lo:hi, :] = jnp.zeros((hi - lo, kvwin.shape[2]), BF16)

    gu[...] = jnp.zeros_like(gu)

    lane = lax.broadcasted_iota(jnp.int32, (p_rows, 2 * head_dim), 1)
    freq = jnp.exp((lane & (head_dim // 2 - 1)).astype(F32) * (-math.log(ROPE_BASE) / (head_dim // 2)))
    sign = jnp.where((lane & (head_dim - 1)) < head_dim // 2, -1.0, 1.0)
    q_row = chip * p_rows + lax.broadcasted_iota(jnp.int32, (p_rows, 2 * head_dim), 0)
    seg = jnp.zeros_like(q_row)
    end = req_ref[0] * 0
    for req in range(side):
        end = end + req_ref[req]
        seg = seg + jnp.where(q_row >= end, req_ref[req], 0)
    angles = (q_row - seg).astype(F32) * freq
    cos_ref[...] = jnp.cos(angles)
    sin_ref[...] = jnp.sin(angles) * sign
    dec_pos = to_column(clen_ref[...], tp * CORES * d_rows, lambda j: (j // (CORES * d_rows)) * d_rows + (j & (d_rows - 1)))
    angles = dec_pos * freq
    cosd_ref[...] = jnp.cos(angles)
    sind_ref[...] = jnp.sin(angles) * sign
    len_ref[...] = to_column(clen_ref[...], tp * CORES * rep * d_rows, lambda j: (j // (CORES * rep * d_rows)) * d_rows + (j & (d_rows - 1))).astype(jnp.int32)
    for piece in range(window // (2 * head_dim)):
        key_row = (chip + 1) * p_rows - window + piece * 2 * head_dim + lane
        mask_ref[:, piece * 2 * head_dim:(piece + 1) * 2 * head_dim] = jnp.where((key_row <= q_row) & (key_row >= seg), 1.0, 0.0)

    pl.semaphore_wait(barrier, side * tp - 1)

    y_local.wait()
    y_far.start()

    @pl.when(x_mine)
    def _():
        x_local.wait()
        x_far.start()

    @pl.when(jnp.logical_not(x_mine))
    def _():
        x_far.wait_recv()

    y_far.wait_recv()
    h_ref[...] = hin[...].astype(F32)

    diag = (lax.broadcasted_iota(jnp.int32, (d_rows, d_rows * head_dim), 1) // head_dim) == lax.broadcasted_iota(jnp.int32, (d_rows, d_rows * head_dim), 0)
    scale = head_dim ** -0.5
    n_peer = tp * CORES

    def exchange(idx, grp):
        sl = at(grp * TILE, TILE, TILE)
        return rc(acc.at[:, sl], xch.at[idx, :, sl], xsend.at[idx, grp], xrecv.at[idx, grp], partner, t_me)

    def settle(idx, grp):
        exchange(idx, grp).wait()
        sl = at(grp * TILE, TILE, TILE)
        h_ref[:, sl] = (h_ref[:, sl] + (acc[:, sl] + xch[idx, :, sl]).astype(BF16).astype(F32)).astype(BF16).astype(F32)

    half_t = tp // CORES
    own_hid = core == t_me // half_t
    piece_me = lax.rem(t_me, half_t) * CORES + core
    n_groups = model // TILE

    def group(ref, base, size, unit, grp):
        return ref.at[at(base, size, unit), at(grp * TILE, TILE, TILE)]

    def hid_src(grp):
        return group(hin, core * half_p, half_p, half_p, grp)

    def hid_dst(grp):
        return group(hid_ref, lax.rem(t_me, half_t) * p_rows + core * half_p, half_p, half_p, grp)

    def hid_local(grp):
        return pltpu.make_async_copy(hid_src(grp), hid_dst(grp), flo.at[0, grp])

    def hid_far(grp, dt):
        return rc(hid_src(grp), hid_dst(grp), fhs.at[grp, dt], fhr.at[grp, piece_me], col * CORES + t_me // half_t, lax.rem(t_me + dt, tp))

    def dec_src(grp):
        return group(hin, p_rows + core * d_rows, d_rows, d_rows, grp)

    def dec_dst(grp):
        return group(dec_ref, t_me * d_rows, d_rows, d_rows, grp)

    def dec_local(grp):
        return pltpu.make_async_copy(dec_src(grp), dec_dst(grp), flo.at[1, grp])

    def dec_far(grp, dt):
        return rc(dec_src(grp), dec_dst(grp), fds.at[grp, dt], fdr.at[grp, dt], s_me, lax.rem(t_me + dt, tp))

    near = (1, tp - 1)

    def send_group(grp):
        sl = at(grp * TILE, TILE, TILE)
        hin[:, sl] = h_ref[:, sl].astype(BF16)
        for dt in near:
            hid_far(grp, dt).start()
            dec_far(grp, dt).start()

        @pl.when(own_hid)
        def _():
            hid_local(grp).start()

        @pl.when(jnp.logical_not(own_hid))
        def _():
            hid_far(grp, 0).start()

        dec_local(grp).start()

    partners = []
    for layer in range(layers):
        w_base = layer * n_w
        norm_ref[...] = rms(h_ref[...])
        cos = cos_ref[...]
        sin = sin_ref[...]

        wait_all(w_copies(w_base))
        out = jnp.dot(norm_ref[...], wbuf[(w_base) % W_SLOTS], preferred_element_type=F32).astype(BF16)
        w_next(w_base)
        qkv[:, q_loc:] = out
        kvwin[layer, window - p_rows:, 0:kv_loc] = rope_tile(out[:p_rows, :kv_loc], cos, sin, head_dim)
        kvwin[layer, window - p_rows:, kv_loc:] = out[:p_rows, kv_loc:]

        def halo(dist):
            target = chip + dist
            last = window - p_rows * dist
            size = p_rows if last - p_rows >= half_p else half_p
            src = kvwin.at[layer, pl.ds(window - size, size), :]
            dst = kvwin.at[layer, pl.ds(last - size, size), :]
            return rc(src, dst, kvs.at[layer, dist - 1], kvr.at[layer, dist - 1], CORES * (target // tp) + core, lax.rem(target, tp))

        for dist in range(1, window // p_rows):
            if dist <= 2:
                @pl.when(chip + dist < chips)
                def _():
                    halo(dist).start()

        for tile in range(n_q):
            idx = w_base + 1 + tile
            wait_all(w_copies(idx))
            out = jnp.dot(norm_ref[...], wbuf[idx % W_SLOTS], preferred_element_type=F32).astype(BF16)
            w_next(idx)
            sl = slice(tile * TILE, (tile + 1) * TILE)
            qkv[:p_rows, sl] = rope_tile(out[:p_rows], cos, sin, head_dim)
            qkv[p_rows:, sl] = out[p_rows:]

        for sub in range(CORES):
            for head in range(heads):
                r0 = p_rows + sub * d_rows
                kk = qkv[r0:r0 + d_rows, q_loc + head * head_dim:q_loc + (head + 1) * head_dim]
                vv = qkv[r0:r0 + d_rows, q_loc + kv_loc + head * head_dim:q_loc + kv_loc + (head + 1) * head_dim]
                dsend[layer, sub, head, :, 0:group_w] = qkv[r0:r0 + d_rows, head * group_w:(head + 1) * group_w]
                dsend[layer, sub, head, :, group_w:] = jnp.concatenate([kk, vv], axis=1)

        def forward(dt, dc):
            s2 = lax.rem(core + dc, CORES)
            t2 = lax.rem(t_me + dt, tp)
            return rc(dsend.at[layer, s2, t2], rdec.at[layer, t_me, core], dss.at[layer, dt * CORES + dc], dsr.at[layer, dt * CORES + dc], col * CORES + s2, t2)

        peers = [(dt, dc) for dt in range(tp) for dc in range(CORES) if dt or dc]
        for dt, dc in peers:
            forward(dt, dc).start()
        rdec[layer, t_me, core] = dsend[layer, core, t_me]
        for dist in range(1, window // p_rows):
            if dist > 2:
                @pl.when(chip + dist < chips)
                def _():
                    halo(dist).start()

        def backward(dt, dc):
            t2 = lax.rem(t_me + tp - dt, tp)
            c2 = lax.rem(core + dc, CORES)
            dst = ctx.at[layer, at(p_rows + core * d_rows, d_rows, d_rows), at(t_me * group_w, group_w, group_w)]
            return rc(cback.at[layer, t2 * CORES + c2], dst, cbs.at[layer, dt * CORES + dc], cbr.at[layer, dt * CORES + dc], col * CORES + c2, t2)

        wait_all(cache_copies(layer))
        for dt, dc in peers:
            forward(dt, dc).wait_recv()
        raw = jnp.concatenate([rdec[layer, p // CORES, p % CORES] for p in range(n_peer)], axis=0)
        roped = rope_tile(raw, cosd_ref[...], sind_ref[...], head_dim)
        q_wide = roped[:, :group_w].astype(F32) * scale
        k_new = roped[:, group_w:group_w + head_dim].astype(F32)
        v_new = raw[:, group_w + head_dim:].astype(F32)
        eye = jnp.where(lax.broadcasted_iota(jnp.int32, (d_rows, d_rows), 0) == lax.broadcasted_iota(jnp.int32, (d_rows, d_rows), 1), 1.0, 0.0).astype(BF16)
        both = jnp.concatenate([k_new, v_new], axis=1).astype(BF16)
        scores = []
        fresh = []
        for p in range(n_peer):
            rs = slice(p * d_rows, (p + 1) * d_rows)
            knv_ref[layer, p // CORES, p % CORES] = lax.dot_general(both[rs], eye, (((0,), (0,)), ((), ())), preferred_element_type=F32).astype(BF16)
            q_parts = [q_wide[rs, r * head_dim:(r + 1) * head_dim] for r in range(rep)]
            pairs = [jnp.concatenate([part, part], axis=1) for part in q_parts]
            lhs = jnp.concatenate([jnp.where(diag, jnp.concatenate([pair] * (d_rows // 2), axis=1), 0.0) for pair in pairs], axis=0).astype(BF16)
            y2 = p // CORES
            k_part = kbuf[y2 * d_rows:(y2 + 1) * d_rows, p % CORES].reshape(d_rows * head_dim, kbuf.shape[3])
            scores.append(jnp.dot(lhs, k_part, preferred_element_type=F32))
            fresh.append(jnp.concatenate(q_parts, axis=0) * jnp.concatenate([k_new[rs]] * rep, axis=0))
        scores = jnp.concatenate(scores, axis=0)
        s_new = jnp.sum(jnp.concatenate(fresh, axis=0), axis=-1, keepdims=True)
        where_new = len_ref[...]
        pos = lax.broadcasted_iota(jnp.int32, scores.shape, 1)
        scores = jnp.where(pos < where_new, scores, -1e30)
        scores = jnp.where(pos == where_new, s_new, scores)
        scores = jnp.exp(scores - jnp.max(scores, axis=-1, keepdims=True))
        prob = (scores * (1.0 / jnp.sum(scores, axis=-1, keepdims=True))).astype(BF16).astype(F32)
        p_new = jnp.sum(jnp.where(pos == where_new, prob, 0.0), axis=-1, keepdims=True)
        p_old = jnp.where(pos == where_new, 0.0, prob).astype(BF16)
        grp_rows = rep * d_rows
        for p in range(n_peer):
            y2 = p // CORES
            gs = slice(p * grp_rows, (p + 1) * grp_rows)
            v_part = vbuf[y2 * d_rows:(y2 + 1) * d_rows, p % CORES].reshape(d_rows * head_dim, vbuf.shape[3])
            full = lax.dot_general(p_old[gs], v_part, NT, preferred_element_type=F32)
            full = jnp.where(jnp.concatenate([diag] * rep, axis=0), full, 0.0)
            fold = full[:, 0:128]
            for piece in range(1, full.shape[1] // 128):
                fold = fold + full[:, piece * 128:(piece + 1) * 128]
            got = fold[:, :head_dim] + fold[:, head_dim:] + p_new[gs] * jnp.concatenate([v_new[p * d_rows:(p + 1) * d_rows]] * rep, axis=0)
            cback[layer, p] = jnp.concatenate([got[r * d_rows:(r + 1) * d_rows] for r in range(rep)], axis=1).astype(BF16)
        for dt, dc in peers:
            backward(dt, dc).start()
        ctx[layer, at(p_rows + core * d_rows, d_rows, d_rows), at(t_me * group_w, group_w, group_w)] = cback[layer, t_me * CORES + core]
        if layer + 1 < layers:
            start_all(cache_copies(layer + 1))

        for dist in range(1, window // p_rows):
            @pl.when(chip >= dist)
            def _():
                halo(dist).wait_recv()

        allowed = mask_ref[...] > 0.5
        for head in range(heads):
            k_head = kvwin[layer, :, head * head_dim:(head + 1) * head_dim]
            v_head = kvwin[layer, :, kv_loc + head * head_dim:kv_loc + (head + 1) * head_dim]
            q0 = head * group_w
            outs = []
            for pair in range(rep // 2):
                q_part = jnp.concatenate([qkv[:p_rows, q0 + sub * head_dim:q0 + (sub + 1) * head_dim] for sub in (2 * pair, 2 * pair + 1)], axis=0)
                q_part = (q_part.astype(F32) * scale).astype(BF16)
                scores = lax.dot_general(q_part, k_head, NT, preferred_element_type=F32).reshape(2, p_rows, window)
                scores = jnp.where(allowed[None], scores, -1e30)
                scores = jnp.exp(scores - jnp.max(scores, axis=-1, keepdims=True))
                prob = (scores * (1.0 / jnp.sum(scores, axis=-1, keepdims=True))).astype(BF16).reshape(2 * p_rows, window)
                got = jnp.dot(prob, v_head, preferred_element_type=F32).astype(BF16)
                outs += [got[:p_rows], got[p_rows:]]
            ctx[layer, 0:p_rows, q0:q0 + group_w] = jnp.concatenate(outs, axis=1)
            isend[layer, head] = jnp.concatenate([k_head[window - p_rows:], v_head[window - p_rows:]], axis=1)

        def spread(dt):
            t2 = lax.rem(t_me + dt, tp)
            return rc(isend.at[layer, t2], inst_ref.at[layer, core, at(chip * p_rows, p_rows, p_rows), :], i1s.at[layer, dt], i1r.at[layer, dt], s_me, t2)

        def keep_own():
            return pltpu.make_async_copy(isend.at[layer, t_me], inst_ref.at[layer, core, at(chip * p_rows, p_rows, p_rows), :], ilo.at[layer])

        def across(dx):
            part = inst_ref.at[layer, core, at(col * tp * p_rows, tp * p_rows, tp * p_rows), :]
            return rc(part, part, i2s.at[layer, dx], i2r.at[layer, dx], lax.rem(col + dx, side // CORES) * CORES + core, t_me)

        def to_partner(layer=layer):
            return rc(inst_ref.at[layer, core], inst_ref.at[layer, core], i3s.at[layer], i3r.at[layer], partner, t_me)

        partners.append(to_partner)
        for dt in range(1, tp):
            spread(dt).start()
        keep_own().start()
        for dt, dc in peers:
            backward(dt, dc).wait_recv()

        for tile in range(n_o):
            idx = w_base + base_o + tile
            wait_all(w_copies(idx))
            for part in range(2):
                lo = (2 * tile + part) * TILE
                acc[:, lo:lo + TILE] = jnp.dot(ctx[layer], wbuf[idx % W_SLOTS, part * q_loc:(part + 1) * q_loc, :], preferred_element_type=F32)
                exchange(2 * layer, 2 * tile + part).start()
            w_next(idx)
        for grp in range(n_groups):
            settle(2 * layer, grp)
        norm_ref[...] = rms(h_ref[...])

        for dt in range(1, tp):
            spread(dt).wait()
        keep_own().wait()
        for dx in range(1, side // CORES):
            across(dx).start()

        def wait_slot(slot):
            pltpu.make_async_copy(wg_ref.at[layer, :, pl.ds(0, TILE)], wbuf.at[slot], wsem.at[slot, 0]).wait()

        def silu_mul(chunk):
            act_ref[:, at(chunk * TILE, TILE, TILE)] = (jax.nn.silu(gu[0].astype(F32)) * gu[1].astype(F32)).astype(BF16)

        def gate_up(chunk, carry):
            slot_g = lax.rem(w_base + base_g + 2 * chunk, W_SLOTS)
            slot_u = lax.rem(w_base + base_g + 2 * chunk + 1, W_SLOTS)
            wait_slot(slot_g)
            wait_slot(slot_u)
            gate = jnp.dot(norm_ref[...], wbuf[slot_g], preferred_element_type=F32).astype(BF16)
            silu_mul(jnp.maximum(chunk - 1, 0))
            upper = jnp.dot(norm_ref[...], wbuf[slot_u], preferred_element_type=F32).astype(BF16)
            gu[0] = gate
            gu[1] = upper
            for which in range(n_ff):
                @pl.when(chunk == which)
                def _():
                    w_next(w_base + base_g + 2 * which)
                    w_next(w_base + base_g + 2 * which + 1)
            return carry

        lax.fori_loop(0, n_ff, gate_up, 0)
        silu_mul(n_ff - 1)

        last = layer + 1 == layers

        def down(tile, carry):
            total = None
            for deep in range(n_deep):
                slot = lax.rem(w_base + base_d + tile * n_deep + deep, W_SLOTS)
                wait_slot(slot)
                part = jnp.dot(act_ref[:, deep * model:(deep + 1) * model], wbuf[slot], preferred_element_type=F32)
                total = part if total is None else total + part
            acc[:, at(tile * TILE, TILE, TILE)] = total
            exchange(2 * layer + 1, tile).start()
            for which in range(n_dn):
                @pl.when(tile == which)
                def _():
                    for deep in range(n_deep):
                        w_next(w_base + base_d + which * n_deep + deep)

            @pl.when(tile > 0)
            def _():
                settle(2 * layer + 1, tile - 1)
                if last:
                    send_group(tile - 1)
            return carry

        lax.fori_loop(0, n_dn, down, 0)
        settle(2 * layer + 1, n_dn - 1)
        if last:
            send_group(n_dn - 1)

        for dist in range(1, window // p_rows):
            @pl.when(chip + dist < chips)
            def _():
                halo(dist).wait_send()
        for dt, dc in peers:
            forward(dt, dc).wait_send()
            backward(dt, dc).wait_send()
        for dx in range(1, side // CORES):
            across(dx).wait()
        to_partner().start()
        if layer == 0:
            @pl.when(x_mine)
            def _():
                x_far.wait_send()

            y_far.wait_send()

    def hid_piece(grp, sub, c2):
        return hid_ref.at[pl.ds(sub * p_rows + c2 * half_p, half_p), pl.ds(grp * TILE, TILE)]

    def hid_pass(grp, sub, c2):
        return rc(hid_piece(grp, sub, c2), hid_piece(grp, sub, c2), hws.at[grp, sub * CORES + c2], fhr.at[grp, sub * CORES + c2], s_me, lax.rem(t_me + near[grp % 2], tp))

    def dec_pass(grp):
        piece = group(dec_ref, lax.rem(t_me + tp - near[grp % 2], tp) * d_rows, d_rows, d_rows, grp)
        return rc(piece, piece, dws.at[grp], fdr.at[grp, 2], s_me, lax.rem(t_me + near[grp % 2], tp))

    def origin(sub):
        return lax.rem(t_me + tp - (core * half_t + sub), tp)

    direct = [(sub, c2) for sub in range(half_t) for c2 in range(CORES)]
    for grp in range(n_groups):
        for sub, c2 in direct:
            gap = origin(sub)

            @pl.when((gap != 2) & jnp.logical_not((gap == 0) & (core == c2)))
            def _():
                hid_pass(grp, sub, c2).wait_recv()

            @pl.when(gap == near[grp % 2])
            def _():
                hid_pass(grp, sub, c2).start()

        dec_far(grp, near[grp % 2]).wait_recv()
        dec_pass(grp).start()
    for grp in range(n_groups):
        dec_far(grp, near[1 - grp % 2]).wait_recv()
        dec_far(grp, 2).wait_recv()
        for sub, c2 in direct:
            gap = origin(sub)

            @pl.when(gap == 2)
            def _():
                hid_pass(grp, sub, c2).wait_recv()

            @pl.when(gap == near[grp % 2])
            def _():
                hid_pass(grp, sub, c2).wait_send()

        dec_pass(grp).wait_send()
        for dt in near:
            hid_far(grp, dt).wait_send()
            dec_far(grp, dt).wait_send()

        @pl.when(own_hid)
        def _():
            hid_local(grp).wait()

        @pl.when(jnp.logical_not(own_hid))
        def _():
            hid_far(grp, 0).wait_send()

        dec_local(grp).wait()
    for handed in partners:
        handed().wait()


def finish_kernel(req_ref, dest_ref, len_ref, knv_ref, hid_ref, dec_ref, inst_ref, k_ref, v_ref,
                  hout_ref, dout_ref, kp_ref, vp_ref, kout_ref, vout_ref, kv_buf, ibuf, hbuf, dbuf, ksem, isem, hsem):
    layers, tp, slots, wide, batch = knv_ref.shape
    head_dim = wide // 2
    t_len = kv_buf.shape[5]
    win = ibuf.shape[2]
    max_req = kp_ref.shape[2]
    s_me = lax.axis_index('side')
    chunks = [(layer, part) for layer in range(layers) for part in range(tp)]

    def caches(num, which, out):
        layer, part = chunks[num]
        far = ((k_ref, v_ref), (kout_ref, vout_ref))[out][which].at[layer, pl.ds(part * batch, batch)]
        near = kv_buf.at[num, which]
        return pltpu.make_async_copy(near, far, ksem.at[num, which, 1]) if out else pltpu.make_async_copy(far, near, ksem.at[num, which, 0])

    cum = req_ref[0] * 0
    start = cum
    length = cum
    for req in range(req_ref.shape[0]):
        start = jnp.where(dest_ref[req] == s_me, cum, start)
        length = jnp.where(dest_ref[req] == s_me, req_ref[req], length)
        cum = cum + req_ref[req]
    blk = jnp.minimum((start // 64) * 64, inst_ref.shape[2] - win)
    grabs = [pltpu.make_async_copy(inst_ref.at[layer, :, pl.ds(pl.multiple_of(blk, 64), win), :], ibuf.at[layer], isem.at[layer]) for layer in range(layers)]
    for num in range(len(chunks)):
        for which in range(2):
            caches(num, which, 0).start()
        if num == 1:
            for one in grabs:
                one.start()
    h_in = [pltpu.make_async_copy(hid_ref, hbuf, hsem.at[0]), pltpu.make_async_copy(dec_ref, dbuf, hsem.at[1])]
    h_out = [pltpu.make_async_copy(hbuf, hout_ref, hsem.at[2]), pltpu.make_async_copy(dbuf, dout_ref, hsem.at[3])]
    for one in h_in:
        one.start()
    row = blk + lax.broadcasted_iota(jnp.int32, (win, max_req), 0)
    want = lax.broadcasted_iota(jnp.int32, (win, max_req), 1)
    pick = jnp.where((row - start == want) & (want < length), 1.0, 0.0).astype(BF16)
    t_iota = lax.broadcasted_iota(jnp.int32, (batch, t_len), 1)
    b_iota = lax.broadcasted_iota(jnp.int32, (batch, t_len), 0)
    for num, (layer, part) in enumerate(chunks):
        spots = [t_iota == len_ref[part * batch + b] for b in range(batch)]
        put = jnp.concatenate([jnp.where(spots[b] & (b_iota == b), 1.0, 0.0).astype(BF16) for b in range(batch)], axis=1)
        news = [jnp.dot(knv_ref[layer, part, slot], put, preferred_element_type=F32) for slot in range(slots)]
        for which in range(2):
            caches(num, which, 0).wait()
        for slot in range(slots):
            for b in range(batch):
                here = jnp.where(spots[b], 1.0, 0.0)
                here = jnp.concatenate([here] * (head_dim // batch), axis=0).astype(BF16) > 0
                new = news[slot][:, b * t_len:(b + 1) * t_len].astype(BF16)
                for which in range(2):
                    kv_buf[num, which, b, slot] = jnp.where(here, new[which * head_dim:(which + 1) * head_dim], kv_buf[num, which, b, slot])
        for which in range(2):
            caches(num, which, 1).start()
        if part == 1:
            grabs[layer].wait()
            for slot in range(slots):
                both = lax.dot_general(ibuf[layer, slot], pick, (((0,), (0,)), ((), ())), preferred_element_type=F32).astype(BF16)
                kp_ref[layer, slot * head_dim:(slot + 1) * head_dim, :] = both[:head_dim]
                vp_ref[layer, slot * head_dim:(slot + 1) * head_dim, :] = both[head_dim:]
    for one in h_in:
        one.wait()
    for one in h_out:
        one.start()
    for num in range(len(chunks)):
        for which in range(2):
            caches(num, which, 1).wait()
    for one in h_out:
        one.wait()


def solution(mesh):
    tp = mesh.shape['tp']
    side = mesh.shape['side']
    rows_spec = P(('pair', 'side'), None)
    batch_spec = P(('pair', 'side'), None, None)
    cache_spec = P(('pair', 'side'), None, None, None, 'tp', None)
    prompt_spec = P(('pair', 'side'), None, None, 'tp', None)

    def local_step(x_loc, req_len, dest, w_qkv, w_out, w_gate, w_up, w_down, y_loc, kc_loc, vc_loc, clen_loc):
        layers = w_qkv.shape[0]
        head_dim = kc_loc.shape[-1]
        slots = kc_loc.shape[-2]
        t_len = kc_loc.shape[3]
        batch = y_loc.shape[1]
        kv_heads = slots * tp
        rep = w_out.shape[1] // head_dim // kv_heads
        model = x_loc.shape[1]
        prompt_rows = x_loc.shape[0]
        seq_len = prompt_rows * side
        max_req = 2 * prompt_rows - prompt_rows // 4
        p_rows = prompt_rows * CORES // tp
        d_rows = batch // tp
        rows = p_rows + CORES * d_rows
        q_loc = w_out.shape[1] // CORES
        kv_loc = kv_heads // CORES * head_dim
        heads = kv_heads // CORES
        window = -(-(max_req - 1) // p_rows) * p_rows + p_rows
        group_w = rep * head_dim

        lengths = clen_loc[0]
        kc = jnp.transpose(kc_loc[0], (0, 1, 3, 4, 2))
        vc = jnp.transpose(vc_loc[0], (0, 1, 3, 4, 2))
        ff_loc = w_gate.shape[2] // CORES
        groups = model // TILE

        dma = pltpu.SemaphoreType.DMA
        n_peer = tp * CORES
        hid, dec, inst, knv = pl.pallas_call(
            functools.partial(mega_kernel, (side, tp, layers, head_dim, rep, slots)),
            out_shape=[jax.ShapeDtypeStruct((prompt_rows, model), BF16), jax.ShapeDtypeStruct((batch, model), BF16),
                       jax.ShapeDtypeStruct((layers, CORES, seq_len, 2 * head_dim), BF16),
                       jax.ShapeDtypeStruct((layers, tp, CORES, 2 * head_dim, d_rows), BF16)],
            in_specs=[SMEM, VMEM, ANY, ANY, ANY, ANY, ANY, ANY, ANY, ANY, ANY],
            out_specs=[ANY, ANY, ANY, VMEM],
            scratch_shapes=[
                pltpu.VMEM((W_SLOTS, model, TILE), BF16),
                pltpu.VMEM((rows, model), BF16),
                pltpu.VMEM((rows, model), F32),
                pltpu.VMEM((rows, model), BF16),
                pltpu.VMEM((rows, model), F32),
                pltpu.VMEM((2 * layers, rows, model), F32),
                pltpu.VMEM((rows, q_loc + 2 * kv_loc), BF16),
                pltpu.VMEM((layers, window, 2 * kv_loc), BF16),
                pltpu.VMEM((layers, CORES, heads, d_rows, group_w + 2 * head_dim), BF16),
                pltpu.VMEM((layers, tp, CORES, d_rows, group_w + 2 * head_dim), BF16),
                pltpu.VMEM((layers, n_peer, d_rows, group_w), BF16),
                pltpu.VMEM((layers, rows, q_loc), BF16),
                pltpu.VMEM((layers, heads, p_rows, 2 * head_dim), BF16),
                pltpu.VMEM((batch, slots, head_dim, t_len), BF16),
                pltpu.VMEM((batch, slots, head_dim, t_len), BF16),
                pltpu.VMEM((rows, ff_loc), BF16),
                pltpu.VMEM((2, rows, TILE), BF16),
                pltpu.VMEM((p_rows, window), F32),
                pltpu.VMEM((p_rows, 2 * head_dim), F32), pltpu.VMEM((p_rows, 2 * head_dim), F32),
                pltpu.VMEM((n_peer * d_rows, 2 * head_dim), F32), pltpu.VMEM((n_peer * d_rows, 2 * head_dim), F32),
                pltpu.VMEM((n_peer * rep * d_rows, 1), jnp.int32),
                dma((W_SLOTS, 2)), dma((6,)), dma((2,)),
                dma((2 * layers, groups)), dma((2 * layers, groups)),
                dma((layers, 4)), dma((layers, 4)),
                dma((layers, n_peer)), dma((layers, n_peer)),
                dma((layers, n_peer)), dma((layers, n_peer)),
                dma((layers, tp)), dma((layers, tp)), dma((layers, side // CORES)), dma((layers, side // CORES)), dma((layers,)), dma((layers,)), dma((layers,)),
                dma((groups, tp)), dma((groups, tp)), dma((groups, tp)), dma((groups, tp)), dma((groups, tp)), dma((groups,)), dma((2, groups)),
            ],
            compiler_params=pltpu.CompilerParams(collective_id=0, has_side_effects=True, vmem_limit_bytes=67043328),
            name="mega",
        )(req_len, clen_loc, x_loc, y_loc[0], kc, vc, w_qkv, w_out, w_gate, w_up, w_down)

        win = 512
        hid, dec, kp, vp, k_out, v_out = pl.pallas_call(
            finish_kernel,
            out_shape=[jax.ShapeDtypeStruct(hid.shape, BF16), jax.ShapeDtypeStruct(dec.shape, BF16)]
            + [jax.ShapeDtypeStruct((layers, slots * head_dim, max_req), BF16)] * 2 + [jax.ShapeDtypeStruct(kc.shape, BF16)] * 2,
            in_specs=[SMEM, SMEM, SMEM, VMEM, ANY, ANY, ANY, ANY, ANY],
            out_specs=[ANY, ANY, VMEM, VMEM, ANY, ANY],
            scratch_shapes=[
                pltpu.VMEM((layers * tp, 2, d_rows, slots, head_dim, t_len), BF16),
                pltpu.VMEM((layers, slots, win, 2 * head_dim), BF16),
                pltpu.VMEM(hid.shape, BF16), pltpu.VMEM(dec.shape, BF16),
                dma((layers * tp, 2, 2)), dma((layers,)), dma((4,)),
            ],
            compiler_params=pltpu.CompilerParams(vmem_limit_bytes=67043328),
            name="finish",
        )(req_len, dest, lengths, knv, hid, dec, inst, kc, vc)

        def cache_back(arr):
            return jnp.transpose(arr, (0, 1, 4, 2, 3))[None]

        def prompt_back(arr):
            return jnp.transpose(arr.reshape(layers, slots, head_dim, max_req), (0, 3, 1, 2))[None]

        return hid, dec[None], prompt_back(kp), prompt_back(vp), cache_back(k_out), cache_back(v_out)

    return jax.shard_map(local_step, mesh=mesh,
                         in_specs=(rows_spec, P('pair'), P('pair'), P(), P(), P(), P(), P(), batch_spec, cache_spec, cache_spec, rows_spec),
                         out_specs=(rows_spec, batch_spec, prompt_spec, prompt_spec, cache_spec, cache_spec),
                         check_vma=False)
```

time: 156 us -> 105 us (0.67)
  the two profiles are of different devices: /device:TPU:102 before, /device:TPU:98 now
where the time goes in v3:
time: 105 us; the launch traced here: 103 us
  Pallas kernels  102 us (97%)
    pallas_call x1, Pallas kernels, local_step(): pl.pallas_call(functools.partial(mega_kernel, (side, tp, layers, head_dim...  89.9 us
    pallas_call x1, Pallas kernels, local_step(): pl.pallas_call(finish_kernel, out_shape=[jax.ShapeDtypeStruct(hid.shape,...  12.1 us

profile of v3, /device:TPU:98, one launch (start us, length us, event | category | flops | bytes accessed | tf_op | source)
XLA Modules:
  0.0 102.8 jit_solution(5178996508063527823)
XLA Ops:
  0.6 89.9 %mega.1 = (bf16[256,2048]{1,0:T(8,128)(2,1)}, bf16[64,2048]{1,0:T(8,128)(2,1)}, bf16[2,2,2048,128]{3,2,1,0:T(8,128)(2,1)}, bf16[2,4,2,128,16]{4,3,2,1,0:T(8,128)(2,1)}) custom-call(s32[8]{0:T(128)} %req_ref.3, s32[1,64]{1,0:T(1,128)} %clen_ref.1, bf16[256,2048]{1,0:T(8,128)(2,1)} %x_ref.1, bf16[64,2048]{1,0:T(8,128)(2,1)} %bitcast.29, ...), custom_call_target="tpu_custom_call" | custom-call | tf_op jit(solution)/shard_map/mega/pallas_call | solution.py:682
  90.5 12.1 %finish.1 = (bf16[256,2048]{1,0:T(8,128)(2,1)}, bf16[64,2048]{1,0:T(8,128)(2,1)}, bf16[2,128,448]{2,1,0:T(8,128)(2,1)}, bf16[2,128,448]{2,1,0:T(8,128)(2,1)}, bf...) custom-call(s32[8]{0:T(128)} %req_ref.3, s32[8]{0:T(128)} %dest_ref.1, s32[64]{0:T(128)} %bitcast.30, ...), custom_call_target="tpu_custom_call" | custom-call | tf_op jit(solution)/shard_map/finish/pallas_call | solution.py:724

commit v4 on v3

--- a/solution.py
+++ b/solution.py
@@ -15,6 +15,7 @@
 TILE = 512
 W_SLOTS = 18
 CORES = 2
+HALVES = 1
 ANY = pl.BlockSpec(memory_space=pl.ANY)
 VMEM = pl.BlockSpec(memory_space=pltpu.VMEM)
 SMEM = pl.BlockSpec(memory_space=pltpu.SMEM)
@@ -45,7 +46,7 @@
 def mega_kernel(cfg, req_ref, clen_ref, x_ref, y_ref, kc_ref, vc_ref, wq_ref, wo_ref, wg_ref, wu_ref, wd_ref,
                 hid_ref, dec_ref, inst_ref, knv_ref,
                 wbuf, hin, h_ref, norm_ref, acc, xch, qkv, kvwin, dsend, rdec, cback, ctx, isend, kbuf, vbuf, act_ref, gu, mask_ref, cos_ref, sin_ref, cosd_ref, sind_ref, len_ref,
-                wsem, insem, csem, xsend, xrecv, kvs, kvr, dss, dsr, cbs, cbr, i1s, i1r, i2s, i2r, i3s, i3r, ilo, fhs, fhr, fds, fdr, hws, dws, flo):
+                wsem, insem, csem, xsend, xrecv, kvs, kvr, kfs, dss, dsr, cbs, cbr, i1s, i1r, i2s, i2r, i3s, i3r, ilo, fhs, fhr, fds, fdr, hws, dws, flo):
     side, tp, layers, head_dim, rep, slots = cfg
     s_me = lax.axis_index('side')
     t_me = lax.axis_index('tp')
@@ -147,14 +148,11 @@
             start_all(cache_copies(0))
 
     for layer in range(layers):
-        kvwin[layer, 0:half_p, :] = jnp.zeros((half_p, kvwin.shape[2]), BF16)
         for dist in range(1, window // p_rows):
-            lo = max(window - p_rows * (dist + 1), half_p)
-
             @pl.when(chip < dist)
             def _():
                 hi = window - p_rows * dist
-                kvwin[layer, lo:hi, :] = jnp.zeros((hi - lo, kvwin.shape[2]), BF16)
+                kvwin[layer, hi - p_rows:hi, :] = jnp.zeros((p_rows, kvwin.shape[2]), BF16)
 
     gu[...] = jnp.zeros_like(gu)
 
@@ -274,19 +272,30 @@
         kvwin[layer, window - p_rows:, 0:kv_loc] = rope_tile(out[:p_rows, :kv_loc], cos, sin, head_dim)
         kvwin[layer, window - p_rows:, kv_loc:] = out[:p_rows, kv_loc:]
 
+        def block(dist):
+            hi = window - p_rows * dist
+            return kvwin.at[layer, pl.ds(hi - p_rows, p_rows), :]
+
         def halo(dist):
             target = chip + dist
-            last = window - p_rows * dist
-            size = p_rows if last - p_rows >= half_p else half_p
-            src = kvwin.at[layer, pl.ds(window - size, size), :]
-            dst = kvwin.at[layer, pl.ds(last - size, size), :]
-            return rc(src, dst, kvs.at[layer, dist - 1], kvr.at[layer, dist - 1], CORES * (target // tp) + core, lax.rem(target, tp))
-
-        for dist in range(1, window // p_rows):
-            if dist <= 2:
-                @pl.when(chip + dist < chips)
-                def _():
-                    halo(dist).start()
+            return rc(block(0), block(dist), kvs.at[layer, dist - 1], kvr.at[layer, dist - 1], CORES * (target // tp) + core, lax.rem(target, tp))
+
+        def goes(dist):
+            return col + 1 < side // CORES if dist == tp else t_me + dist < tp
+
+        def hand_on(place):
+            dist = tp + place - t_me
+            hi = window - p_rows * dist
+            dst = kvwin.at[layer, at(hi - p_rows, p_rows, p_rows), :]
+            return rc(block(tp), dst, kfs.at[layer, place], kvr.at[layer, dist - 1], s_me, place)
+
+        def hands_on(place):
+            return (col > 0) & (place < t_me)
+
+        for dist in (tp, 1):
+            @pl.when(goes(dist))
+            def _():
+                halo(dist).start()
 
         for tile in range(n_q):
             idx = w_base + 1 + tile
@@ -314,11 +323,19 @@
         for dt, dc in peers:
             forward(dt, dc).start()
         rdec[layer, t_me, core] = dsend[layer, core, t_me]
-        for dist in range(1, window // p_rows):
-            if dist > 2:
-                @pl.when(chip + dist < chips)
-                def _():
-                    halo(dist).start()
+        for dist in range(2, tp):
+            @pl.when(goes(dist))
+            def _():
+                halo(dist).start()
+
+        @pl.when(col > 0)
+        def _():
+            halo(tp).wait_recv()
+
+        for place in range(tp - 1):
+            @pl.when(hands_on(place))
+            def _():
+                hand_on(place).start()
 
         def backward(dt, dc):
             t2 = lax.rem(t_me + tp - dt, tp)
@@ -376,7 +393,7 @@
         if layer + 1 < layers:
             start_all(cache_copies(layer + 1))
 
-        for dist in range(1, window // p_rows):
+        for dist in range(1, tp):
             @pl.when(chip >= dist)
             def _():
                 halo(dist).wait_recv()
@@ -386,16 +403,14 @@
             k_head = kvwin[layer, :, head * head_dim:(head + 1) * head_dim]
             v_head = kvwin[layer, :, kv_loc + head * head_dim:kv_loc + (head + 1) * head_dim]
             q0 = head * group_w
-            outs = []
-            for pair in range(rep // 2):
-                q_part = jnp.concatenate([qkv[:p_rows, q0 + sub * head_dim:q0 + (sub + 1) * head_dim] for sub in (2 * pair, 2 * pair + 1)], axis=0)
-                q_part = (q_part.astype(F32) * scale).astype(BF16)
-                scores = lax.dot_general(q_part, k_head, NT, preferred_element_type=F32).reshape(2, p_rows, window)
-                scores = jnp.where(allowed[None], scores, -1e30)
-                scores = jnp.exp(scores - jnp.max(scores, axis=-1, keepdims=True))
-                prob = (scores * (1.0 / jnp.sum(scores, axis=-1, keepdims=True))).astype(BF16).reshape(2 * p_rows, window)
-                got = jnp.dot(prob, v_head, preferred_element_type=F32).astype(BF16)
-                outs += [got[:p_rows], got[p_rows:]]
+            q_part = jnp.concatenate([qkv[:p_rows, q0 + sub * head_dim:q0 + (sub + 1) * head_dim] for sub in range(rep)], axis=0)
+            q_part = (q_part.astype(F32) * scale).astype(BF16)
+            scores = lax.dot_general(q_part, k_head, NT, preferred_element_type=F32).reshape(rep, p_rows, window)
+            scores = jnp.where(allowed[None], scores, -1e30)
+            scores = jnp.exp(scores - jnp.max(scores, axis=-1, keepdims=True))
+            prob = (scores * (1.0 / jnp.sum(scores, axis=-1, keepdims=True))).astype(BF16).reshape(rep * p_rows, window)
+            got = jnp.dot(prob, v_head, preferred_element_type=F32).astype(BF16)
+            outs = [got[sub * p_rows:(sub + 1) * p_rows] for sub in range(rep)]
             ctx[layer, 0:p_rows, q0:q0 + group_w] = jnp.concatenate(outs, axis=1)
             isend[layer, head] = jnp.concatenate([k_head[window - p_rows:], v_head[window - p_rows:]], axis=1)
 
@@ -481,22 +496,27 @@
                     for deep in range(n_deep):
                         w_next(w_base + base_d + which * n_deep + deep)
 
-            @pl.when(tile > 0)
-            def _():
-                settle(2 * layer + 1, tile - 1)
+            @pl.when(tile > 1)
+            def _():
+                settle(2 * layer + 1, tile - 2)
                 if last:
-                    send_group(tile - 1)
+                    send_group(tile - 2)
             return carry
 
         lax.fori_loop(0, n_dn, down, 0)
-        settle(2 * layer + 1, n_dn - 1)
-        if last:
-            send_group(n_dn - 1)
-
-        for dist in range(1, window // p_rows):
-            @pl.when(chip + dist < chips)
+        for grp in range(n_dn - 2, n_dn):
+            settle(2 * layer + 1, grp)
+            if last:
+                send_group(grp)
+
+        for dist in range(1, tp + 1):
+            @pl.when(goes(dist))
             def _():
                 halo(dist).wait_send()
+        for place in range(tp - 1):
+            @pl.when(hands_on(place))
+            def _():
+                hand_on(place).wait_send()
         for dt, dc in peers:
             forward(dt, dc).wait_send()
             backward(dt, dc).wait_send()
@@ -570,21 +590,24 @@
         handed().wait()
 
 
-def finish_kernel(req_ref, dest_ref, len_ref, knv_ref, hid_ref, dec_ref, inst_ref, k_ref, v_ref,
-                  hout_ref, dout_ref, kp_ref, vp_ref, kout_ref, vout_ref, kv_buf, ibuf, hbuf, dbuf, ksem, isem, hsem):
+def finish_kernel(req_ref, dest_ref, len_ref, knv_hbm, hid_ref, dec_ref, inst_ref, k_ref, v_ref,
+                  hout_ref, dout_ref, kp_out, vp_out, kout_ref, vout_ref, kv_buf, ibuf, hbuf, dbuf, knv_ref, kp_ref, vp_ref, ksem, isem, hsem):
     layers, tp, slots, wide, batch = knv_ref.shape
     head_dim = wide // 2
     t_len = kv_buf.shape[5]
     win = ibuf.shape[2]
     max_req = kp_ref.shape[2]
     s_me = lax.axis_index('side')
-    chunks = [(layer, part) for layer in range(layers) for part in range(tp)]
-
-    def caches(num, which, out):
-        layer, part = chunks[num]
-        far = ((k_ref, v_ref), (kout_ref, vout_ref))[out][which].at[layer, pl.ds(part * batch, batch)]
-        near = kv_buf.at[num, which]
-        return pltpu.make_async_copy(near, far, ksem.at[num, which, 1]) if out else pltpu.make_async_copy(far, near, ksem.at[num, which, 0])
+    total_b = tp * batch
+    units = [(layer, which, half) for layer in range(layers) for half in range(HALVES) for which in range(2)]
+    part_b = total_b // HALVES
+
+    def caches(num, out):
+        layer, which, half = units[num]
+        rows = pl.ds(half * part_b, part_b)
+        far = ((k_ref, v_ref), (kout_ref, vout_ref))[out][which].at[layer, rows]
+        near = kv_buf.at[layer, which, rows]
+        return pltpu.make_async_copy(near, far, ksem.at[num, 1]) if out else pltpu.make_async_copy(far, near, ksem.at[num, 0])
 
     cum = req_ref[0] * 0
     start = cum
@@ -595,12 +618,13 @@
         cum = cum + req_ref[req]
     blk = jnp.minimum((start // 64) * 64, inst_ref.shape[2] - win)
     grabs = [pltpu.make_async_copy(inst_ref.at[layer, :, pl.ds(pl.multiple_of(blk, 64), win), :], ibuf.at[layer], isem.at[layer]) for layer in range(layers)]
-    for num in range(len(chunks)):
-        for which in range(2):
-            caches(num, which, 0).start()
-        if num == 1:
-            for one in grabs:
-                one.start()
+    knv_in = pltpu.make_async_copy(knv_hbm, knv_ref, hsem.at[4])
+    prompt_out = [pltpu.make_async_copy(kp_ref, kp_out, hsem.at[5]), pltpu.make_async_copy(vp_ref, vp_out, hsem.at[6])]
+    for one in grabs:
+        one.start()
+    knv_in.start()
+    for num in range(len(units)):
+        caches(num, 0).start()
     h_in = [pltpu.make_async_copy(hid_ref, hbuf, hsem.at[0]), pltpu.make_async_copy(dec_ref, dbuf, hsem.at[1])]
     h_out = [pltpu.make_async_copy(hbuf, hout_ref, hsem.at[2]), pltpu.make_async_copy(dbuf, dout_ref, hsem.at[3])]
     for one in h_in:
@@ -608,37 +632,31 @@
     row = blk + lax.broadcasted_iota(jnp.int32, (win, max_req), 0)
     want = lax.broadcasted_iota(jnp.int32, (win, max_req), 1)
     pick = jnp.where((row - start == want) & (want < length), 1.0, 0.0).astype(BF16)
-    t_iota = lax.broadcasted_iota(jnp.int32, (batch, t_len), 1)
-    b_iota = lax.broadcasted_iota(jnp.int32, (batch, t_len), 0)
-    for num, (layer, part) in enumerate(chunks):
-        spots = [t_iota == len_ref[part * batch + b] for b in range(batch)]
-        put = jnp.concatenate([jnp.where(spots[b] & (b_iota == b), 1.0, 0.0).astype(BF16) for b in range(batch)], axis=1)
-        news = [jnp.dot(knv_ref[layer, part, slot], put, preferred_element_type=F32) for slot in range(slots)]
-        for which in range(2):
-            caches(num, which, 0).wait()
+    for lay in range(layers):
+        grabs[lay].wait()
         for slot in range(slots):
-            for b in range(batch):
-                here = jnp.where(spots[b], 1.0, 0.0)
-                here = jnp.concatenate([here] * (head_dim // batch), axis=0).astype(BF16) > 0
-                new = news[slot][:, b * t_len:(b + 1) * t_len].astype(BF16)
-                for which in range(2):
-                    kv_buf[num, which, b, slot] = jnp.where(here, new[which * head_dim:(which + 1) * head_dim], kv_buf[num, which, b, slot])
-        for which in range(2):
-            caches(num, which, 1).start()
-        if part == 1:
-            grabs[layer].wait()
+            both = lax.dot_general(ibuf[lay, slot], pick, (((0,), (0,)), ((), ())), preferred_element_type=F32).astype(BF16)
+            kp_ref[lay, slot * head_dim:(slot + 1) * head_dim, :] = both[:head_dim]
+            vp_ref[lay, slot * head_dim:(slot + 1) * head_dim, :] = both[head_dim:]
+    for one in prompt_out:
+        one.start()
+    knv_in.wait()
+    t_iota = lax.broadcasted_iota(jnp.int32, (head_dim, t_len), 1)
+    for num, (layer, which, half) in enumerate(units):
+        caches(num, 0).wait()
+        for b in range(half * part_b, (half + 1) * part_b):
+            here = t_iota == len_ref[b]
             for slot in range(slots):
-                both = lax.dot_general(ibuf[layer, slot], pick, (((0,), (0,)), ((), ())), preferred_element_type=F32).astype(BF16)
-                kp_ref[layer, slot * head_dim:(slot + 1) * head_dim, :] = both[:head_dim]
-                vp_ref[layer, slot * head_dim:(slot + 1) * head_dim, :] = both[head_dim:]
+                new = knv_ref[layer, b // batch, slot, which * head_dim:(which + 1) * head_dim, b % batch:b % batch + 1].astype(F32)
+                kv_buf[layer, which, b, slot] = jnp.where(here, new, kv_buf[layer, which, b, slot].astype(F32)).astype(BF16)
+        caches(num, 1).start()
     for one in h_in:
         one.wait()
     for one in h_out:
         one.start()
-    for num in range(len(chunks)):
-        for which in range(2):
-            caches(num, which, 1).wait()
-    for one in h_out:
+    for num in range(len(units)):
+        caches(num, 1).wait()
+    for one in h_out + prompt_out:
         one.wait()
 
 
@@ -669,6 +687,7 @@
         kv_loc = kv_heads // CORES * head_dim
         heads = kv_heads // CORES
         window = -(-(max_req - 1) // p_rows) * p_rows + p_rows
+        assert window == (tp + 1) * p_rows
         group_w = rep * head_dim
 
         lengths = clen_loc[0]
@@ -710,7 +729,7 @@
                 pltpu.VMEM((n_peer * rep * d_rows, 1), jnp.int32),
                 dma((W_SLOTS, 2)), dma((6,)), dma((2,)),
                 dma((2 * layers, groups)), dma((2 * layers, groups)),
-                dma((layers, 4)), dma((layers, 4)),
+                dma((layers, tp)), dma((layers, tp)), dma((layers, tp)),
                 dma((layers, n_peer)), dma((layers, n_peer)),
                 dma((layers, n_peer)), dma((layers, n_peer)),
                 dma((layers, tp)), dma((layers, tp)), dma((layers, side // CORES)), dma((layers, side // CORES)), dma((layers,)), dma((layers,)), dma((layers,)),
@@ -725,13 +744,14 @@
             finish_kernel,
             out_shape=[jax.ShapeDtypeStruct(hid.shape, BF16), jax.ShapeDtypeStruct(dec.shape, BF16)]
             + [jax.ShapeDtypeStruct((layers, slots * head_dim, max_req), BF16)] * 2 + [jax.ShapeDtypeStruct(kc.shape, BF16)] * 2,
-            in_specs=[SMEM, SMEM, SMEM, VMEM, ANY, ANY, ANY, ANY, ANY],
-            out_specs=[ANY, ANY, VMEM, VMEM, ANY, ANY],
+            in_specs=[SMEM, SMEM, SMEM, ANY, ANY, ANY, ANY, ANY, ANY],
+            out_specs=[ANY] * 6,
             scratch_shapes=[
-                pltpu.VMEM((layers * tp, 2, d_rows, slots, head_dim, t_len), BF16),
+                pltpu.VMEM((layers, 2, batch, slots, head_dim, t_len), BF16),
                 pltpu.VMEM((layers, slots, win, 2 * head_dim), BF16),
-                pltpu.VMEM(hid.shape, BF16), pltpu.VMEM(dec.shape, BF16),
-                dma((layers * tp, 2, 2)), dma((layers,)), dma((4,)),
+                pltpu.VMEM(hid.shape, BF16), pltpu.VMEM(dec.shape, BF16), pltpu.VMEM(knv.shape, BF16),
+                pltpu.VMEM((layers, slots * head_dim, max_req), BF16), pltpu.VMEM((layers, slots * head_dim, max_req), BF16),
+                dma((2 * layers * HALVES, 2)), dma((layers,)), dma((7,)),
             ],
             compiler_params=pltpu.CompilerParams(vmem_limit_bytes=67043328),
             name="finish",

time: 105 us -> 98.1 us (0.934); the launches traced: 103 us -> 97.2 us
  Pallas kernels: 102 us -> 96.3 us
    pallas_call x1, Pallas kernels: 89.9 us -> 87 us  [local_step(): pl.pallas_call(functools.partial(mega_kernel, (side, tp, layers, head_dim...]
    pallas_call x1, Pallas kernels: 12.1 us -> 9.33 us  [local_step(): pl.pallas_call(finish_kernel, out_shape=[jax.ShapeDtypeStruct(hid.shape,...]
where the time goes in v4:
time: 98.1 us; the launch traced here: 97.2 us
  Pallas kernels  96.3 us (98%)
    pallas_call x1, Pallas kernels, local_step(): pl.pallas_call(functools.partial(mega_kernel, (side, tp, layers, head_dim...  87 us
    pallas_call x1, Pallas kernels, local_step(): pl.pallas_call(finish_kernel, out_shape=[jax.ShapeDtypeStruct(hid.shape,...  9.33 us

profile of v4, /device:TPU:98, one launch (start us, length us, event | category | flops | bytes accessed | tf_op | source)
XLA Modules:
  0.0 97.2 jit_solution(4255326341327863569)
XLA Ops:
  0.6 87.0 %mega.1 = (bf16[256,2048]{1,0:T(8,128)(2,1)}, bf16[64,2048]{1,0:T(8,128)(2,1)}, bf16[2,2,2048,128]{3,2,1,0:T(8,128)(2,1)}, bf16[2,4,2,128,16]{4,3,2,1,0:T(8,128)(2,1)}) custom-call(s32[8]{0:T(128)} %req_ref.3, s32[1,64]{1,0:T(1,128)} %clen_ref.1, bf16[256,2048]{1,0:T(8,128)(2,1)} %x_ref.1, bf16[64,2048]{1,0:T(8,128)(2,1)} %bitcast.29, ...), custom_call_target="tpu_custom_call" | custom-call | tf_op jit(solution)/shard_map/mega/pallas_call | solution.py:701
  87.7 9.3 %finish.1 = (bf16[256,2048]{1,0:T(8,128)(2,1)}, bf16[64,2048]{1,0:T(8,128)(2,1)}, bf16[2,128,448]{2,1,0:T(8,128)(2,1)}, bf16[2,128,448]{2,1,0:T(8,128)(2,1)}, bf...) custom-call(s32[8]{0:T(128)} %req_ref.3, s32[8]{0:T(128)} %dest_ref.1, s32[64]{0:T(128)} %bitcast.30, ...), custom_call_target="tpu_custom_call" | custom-call | tf_op jit(solution)/shard_map/finish/pallas_call | solution.py:743

commit v5 on v4

--- a/solution.py
+++ b/solution.py
@@ -259,6 +259,7 @@
         dec_local(grp).start()
 
     partners = []
+    crossed = []
     for layer in range(layers):
         w_base = layer * n_w
         norm_ref[...] = rms(h_ref[...])
@@ -272,22 +273,20 @@
         kvwin[layer, window - p_rows:, 0:kv_loc] = rope_tile(out[:p_rows, :kv_loc], cos, sin, head_dim)
         kvwin[layer, window - p_rows:, kv_loc:] = out[:p_rows, kv_loc:]
 
-        def block(dist):
-            hi = window - p_rows * dist
-            return kvwin.at[layer, pl.ds(hi - p_rows, p_rows), :]
-
-        def halo(dist):
+        def block(base, part):
+            return kvwin.at[layer, at(base, p_rows, p_rows), pl.ds(part * kv_loc, kv_loc)]
+
+        def halo(dist, part):
             target = chip + dist
-            return rc(block(0), block(dist), kvs.at[layer, dist - 1], kvr.at[layer, dist - 1], CORES * (target // tp) + core, lax.rem(target, tp))
+            return rc(block(window - p_rows, part), block(window - p_rows * (dist + 1), part), kvs.at[layer, dist - 1, part], kvr.at[layer, dist - 1, part],
+                      CORES * (target // tp) + core, lax.rem(target, tp))
 
         def goes(dist):
             return col + 1 < side // CORES if dist == tp else t_me + dist < tp
 
-        def hand_on(place):
+        def hand_on(place, part):
             dist = tp + place - t_me
-            hi = window - p_rows * dist
-            dst = kvwin.at[layer, at(hi - p_rows, p_rows, p_rows), :]
-            return rc(block(tp), dst, kfs.at[layer, place], kvr.at[layer, dist - 1], s_me, place)
+            return rc(block(0, part), block(window - p_rows * (dist + 1), part), kfs.at[layer, place, part], kvr.at[layer, dist - 1, part], s_me, place)
 
         def hands_on(place):
             return (col > 0) & (place < t_me)
@@ -295,7 +294,8 @@
         for dist in (tp, 1):
             @pl.when(goes(dist))
             def _():
-                halo(dist).start()
+                for part in range(2):
+                    halo(dist, part).start()
 
         for tile in range(n_q):
             idx = w_base + 1 + tile
@@ -326,16 +326,18 @@
         for dist in range(2, tp):
             @pl.when(goes(dist))
             def _():
-                halo(dist).start()
-
-        @pl.when(col > 0)
-        def _():
-            halo(tp).wait_recv()
-
-        for place in range(tp - 1):
-            @pl.when(hands_on(place))
-            def _():
-                hand_on(place).start()
+                for part in range(2):
+                    halo(dist, part).start()
+
+        for part in range(2):
+            @pl.when(col > 0)
+            def _():
+                halo(tp, part).wait_recv()
+
+            for place in range(tp - 1):
+                @pl.when(hands_on(place))
+                def _():
+                    hand_on(place, part).start()
 
         def backward(dt, dc):
             t2 = lax.rem(t_me + tp - dt, tp)
@@ -396,7 +398,8 @@
         for dist in range(1, tp):
             @pl.when(chip >= dist)
             def _():
-                halo(dist).wait_recv()
+                for part in range(2):
+                    halo(dist, part).wait_recv()
 
         allowed = mask_ref[...] > 0.5
         for head in range(heads):
@@ -421,14 +424,20 @@
         def keep_own():
             return pltpu.make_async_copy(isend.at[layer, t_me], inst_ref.at[layer, core, at(chip * p_rows, p_rows, p_rows), :], ilo.at[layer])
 
-        def across(dx):
+        def across(dx, layer=layer):
             part = inst_ref.at[layer, core, at(col * tp * p_rows, tp * p_rows, tp * p_rows), :]
             return rc(part, part, i2s.at[layer, dx], i2r.at[layer, dx], lax.rem(col + dx, side // CORES) * CORES + core, t_me)
 
         def to_partner(layer=layer):
             return rc(inst_ref.at[layer, core], inst_ref.at[layer, core], i3s.at[layer], i3r.at[layer], partner, t_me)
 
+        def pass_on(across=across, to_partner=to_partner):
+            for dx in range(1, side // CORES):
+                across(dx).wait()
+            to_partner().start()
+
         partners.append(to_partner)
+        crossed.append(pass_on)
         for dt in range(1, tp):
             spread(dt).start()
         keep_own().start()
@@ -446,12 +455,6 @@
         for grp in range(n_groups):
             settle(2 * layer, grp)
         norm_ref[...] = rms(h_ref[...])
-
-        for dt in range(1, tp):
-            spread(dt).wait()
-        keep_own().wait()
-        for dx in range(1, side // CORES):
-            across(dx).start()
 
         def wait_slot(slot):
             pltpu.make_async_copy(wg_ref.at[layer, :, pl.ds(0, TILE)], wbuf.at[slot], wsem.at[slot, 0]).wait()
@@ -478,6 +481,13 @@
 
         lax.fori_loop(0, n_ff, gate_up, 0)
         silu_mul(n_ff - 1)
+        if layer:
+            crossed[layer - 1]()
+        for dt in range(1, tp):
+            spread(dt).wait()
+        keep_own().wait()
+        for dx in range(1, side // CORES):
+            across(dx).start()
 
         last = layer + 1 == layers
 
@@ -512,17 +522,16 @@
         for dist in range(1, tp + 1):
             @pl.when(goes(dist))
             def _():
-                halo(dist).wait_send()
+                for part in range(2):
+                    halo(dist, part).wait_send()
         for place in range(tp - 1):
             @pl.when(hands_on(place))
             def _():
-                hand_on(place).wait_send()
+                for part in range(2):
+                    hand_on(place, part).wait_send()
         for dt, dc in peers:
             forward(dt, dc).wait_send()
             backward(dt, dc).wait_send()
-        for dx in range(1, side // CORES):
-            across(dx).wait()
-        to_partner().start()
         if layer == 0:
             @pl.when(x_mine)
             def _():
@@ -558,6 +567,7 @@
 
         dec_far(grp, near[grp % 2]).wait_recv()
         dec_pass(grp).start()
+    crossed[-1]()
     for grp in range(n_groups):
         dec_far(grp, near[1 - grp % 2]).wait_recv()
         dec_far(grp, 2).wait_recv()
@@ -620,36 +630,40 @@
     grabs = [pltpu.make_async_copy(inst_ref.at[layer, :, pl.ds(pl.multiple_of(blk, 64), win), :], ibuf.at[layer], isem.at[layer]) for layer in range(layers)]
     knv_in = pltpu.make_async_copy(knv_hbm, knv_ref, hsem.at[4])
     prompt_out = [pltpu.make_async_copy(kp_ref, kp_out, hsem.at[5]), pltpu.make_async_copy(vp_ref, vp_out, hsem.at[6])]
+    knv_in.start()
+    for num in range(2):
+        caches(num, 0).start()
     for one in grabs:
         one.start()
-    knv_in.start()
-    for num in range(len(units)):
-        caches(num, 0).start()
     h_in = [pltpu.make_async_copy(hid_ref, hbuf, hsem.at[0]), pltpu.make_async_copy(dec_ref, dbuf, hsem.at[1])]
     h_out = [pltpu.make_async_copy(hbuf, hout_ref, hsem.at[2]), pltpu.make_async_copy(dbuf, dout_ref, hsem.at[3])]
-    for one in h_in:
-        one.start()
     row = blk + lax.broadcasted_iota(jnp.int32, (win, max_req), 0)
     want = lax.broadcasted_iota(jnp.int32, (win, max_req), 1)
     pick = jnp.where((row - start == want) & (want < length), 1.0, 0.0).astype(BF16)
-    for lay in range(layers):
-        grabs[lay].wait()
-        for slot in range(slots):
-            both = lax.dot_general(ibuf[lay, slot], pick, (((0,), (0,)), ((), ())), preferred_element_type=F32).astype(BF16)
-            kp_ref[lay, slot * head_dim:(slot + 1) * head_dim, :] = both[:head_dim]
-            vp_ref[lay, slot * head_dim:(slot + 1) * head_dim, :] = both[head_dim:]
-    for one in prompt_out:
-        one.start()
     knv_in.wait()
     t_iota = lax.broadcasted_iota(jnp.int32, (head_dim, t_len), 1)
     for num, (layer, which, half) in enumerate(units):
         caches(num, 0).wait()
+        if num + 2 < len(units):
+            caches(num + 2, 0).start()
+            if num == 1:
+                for one in h_in:
+                    one.start()
         for b in range(half * part_b, (half + 1) * part_b):
             here = t_iota == len_ref[b]
             for slot in range(slots):
                 new = knv_ref[layer, b // batch, slot, which * head_dim:(which + 1) * head_dim, b % batch:b % batch + 1].astype(F32)
                 kv_buf[layer, which, b, slot] = jnp.where(here, new, kv_buf[layer, which, b, slot].astype(F32)).astype(BF16)
         caches(num, 1).start()
+        if num == 1:
+            for lay in range(layers):
+                grabs[lay].wait()
+                for slot in range(slots):
+                    both = lax.dot_general(ibuf[lay, slot], pick, (((0,), (0,)), ((), ())), preferred_element_type=F32).astype(BF16)
+                    kp_ref[lay, slot * head_dim:(slot + 1) * head_dim, :] = both[:head_dim]
+                    vp_ref[lay, slot * head_dim:(slot + 1) * head_dim, :] = both[head_dim:]
+            for one in prompt_out:
+                one.start()
     for one in h_in:
         one.wait()
     for one in h_out:
@@ -729,7 +743,7 @@
                 pltpu.VMEM((n_peer * rep * d_rows, 1), jnp.int32),
                 dma((W_SLOTS, 2)), dma((6,)), dma((2,)),
                 dma((2 * layers, groups)), dma((2 * layers, groups)),
-                dma((layers, tp)), dma((layers, tp)), dma((layers, tp)),
+                dma((layers, tp, 2)), dma((layers, tp, 2)), dma((layers, tp, 2)),
                 dma((layers, n_peer)), dma((layers, n_peer)),
                 dma((layers, n_peer)), dma((layers, n_peer)),
                 dma((layers, tp)), dma((layers, tp)), dma((layers, side // CORES)), dma((layers, side // CORES)), dma((layers,)), dma((layers,)), dma((layers,)),

time: 98.1 us -> 96 us (0.979)
  Pallas kernels: 96.3 us -> 93.9 us
    pallas_call x1, Pallas kernels: 87 us -> 84.9 us  [local_step(): pl.pallas_call(functools.partial(mega_kernel, (side, tp, layers, head_dim...]
where the time goes in v5:
time: 96 us; the launch traced here: 94.8 us
  Pallas kernels  93.9 us (98%)
    pallas_call x1, Pallas kernels, local_step(): pl.pallas_call(functools.partial(mega_kernel, (side, tp, layers, head_dim...  84.9 us
    pallas_call x1, Pallas kernels, local_step(): pl.pallas_call(finish_kernel, out_shape=[jax.ShapeDtypeStruct(hid.shape,...  8.98 us

profile of v5, /device:TPU:98, one launch (start us, length us, event | category | flops | bytes accessed | tf_op | source)
XLA Modules:
  0.0 94.8 jit_solution(6477913291900039262)
XLA Ops:
  0.6 84.9 %mega.1 = (bf16[256,2048]{1,0:T(8,128)(2,1)}, bf16[64,2048]{1,0:T(8,128)(2,1)}, bf16[2,2,2048,128]{3,2,1,0:T(8,128)(2,1)}, bf16[2,4,2,128,16]{4,3,2,1,0:T(8,128)(2,1)}) custom-call(s32[8]{0:T(128)} %req_ref.3, s32[1,64]{1,0:T(1,128)} %clen_ref.1, bf16[256,2048]{1,0:T(8,128)(2,1)} %x_ref.1, bf16[64,2048]{1,0:T(8,128)(2,1)} %bitcast.29, ...), custom_call_target="tpu_custom_call" | custom-call | tf_op jit(solution)/shard_map/mega/pallas_call | solution.py:715
  85.6 9.0 %finish.1 = (bf16[256,2048]{1,0:T(8,128)(2,1)}, bf16[64,2048]{1,0:T(8,128)(2,1)}, bf16[2,128,448]{2,1,0:T(8,128)(2,1)}, bf16[2,128,448]{2,1,0:T(8,128)(2,1)}, bf...) custom-call(s32[8]{0:T(128)} %req_ref.3, s32[8]{0:T(128)} %dest_ref.1, s32[64]{0:T(128)} %bitcast.30, ...), custom_call_target="tpu_custom_call" | custom-call | tf_op jit(solution)/shard_map/finish/pallas_call | solution.py:757
